TPU v7x, 32 devices: a whole 2x2x4 slice. The times are simulated.
32 devices in a mesh: vox: 8 (over y, x, core), sen: 4 (over z).
Axes of the slice: x: 2, y: 2, z: 4, core: 2. Of those that a mesh axis runs over, the one named last changes fastest.
Arguments:
- image: float32 [8, 2, 512], P('vox'), may hold values from -6 to 6
- weights: bfloat16 [8, 4, 5, 1024, 1024], P('vox', 'sen'), may hold values from -0.0625 to 0.0625
- block_ids: int32 [8, 4, 5], P('vox', 'sen'), may hold values from 0 to 15
- offsets: int32 [8, 4, 5], P('vox', 'sen'), may hold values from 0 to 1984
- counts: int32 [8, 4], P('vox', 'sen'), may hold values from 1 to 5, as said below
- measured: bfloat16 [4, 256, 2048], P('sen', 'vox'), may hold values from -6 to 6
Outputs:
- image_next: float32 [8, 2, 512], P('vox')
- residual: float32 [4, 256, 2048], P('sen', 'vox')
Inputs may be any that keep to these rules, and one draw needn't show every extreme that they name: `counts`: some slab and group has all 5 slots live in every draw.
All inputs are finite; a program needn't handle non-finite values.
Results may differ from a plain program's by a relative error of at most 0.0025.
Values may be sent and summed in bfloat16 or wider, within the bound.
A program may use at most 64 MiB of HBM per device.

v0:
```python
import functools

import jax
import jax.numpy as jnp
from jax import lax
from jax.experimental import pallas as pl
from jax.experimental.pallas import tpu as pltpu
from jax.sharding import PartitionSpec as P

SB = 16
WIN = 64
LANES = 128

STEP_SIZE = 0.25
TV_WEIGHT = 0.3
TV_EPS = 0.01
C1 = 8.0 / 12.0
C2 = 1.0 / 12.0
MESH = pl.DeviceIdType.MESH


def lane_iota(shape):
    return lax.broadcasted_iota(jnp.int32, shape, len(shape) - 1)


def ahead(value, shift):
    length = value.shape[-1]
    return pltpu.roll(value, (-shift) % length, value.ndim - 1)


def stencil(value):
    return C2 * ahead(value, -2) - C1 * ahead(value, -1) + C1 * ahead(value, 1) - C2 * ahead(value, 2)


def stencil_edges(value):
    length = value.shape[-1]
    at = lane_iota(value.shape)
    total = jnp.where(at >= 2, C2 * ahead(value, -2), 0.0)
    total = total - jnp.where(at >= 1, C1 * ahead(value, -1), 0.0)
    total = total + jnp.where(at < length - 1, C1 * ahead(value, 1), 0.0)
    return total - jnp.where(at < length - 2, C2 * ahead(value, 2), 0.0)


def block_mask(width):
    row = lax.broadcasted_iota(jnp.int32, (SB, width), 0)
    return lane_iota((SB, width)) // WIN == row


def gather_kernel(
    n, slots, chunks, image_in, weights, ids_in, offs_in, counts,
    pieces_all, meta_all, halo, wbuf,
    image, ids, offs, mine, meta,
    wsem, load_sem, local_sem, small_send, small_recv, halo_send, halo_recv,
    piece_send, piece_recv,
):
    me = lax.axis_index("vox")
    voxels = weights.shape[3]
    depth = voxels // chunks
    groups = mine.shape[0]

    arguments = []
    pairs = ((ids_in, ids), (offs_in, offs), (image_in, image))
    for i, (src, dst) in enumerate(pairs):
        load = pltpu.make_async_copy(src, dst, load_sem.at[i])
        load.start()
        arguments.append(load)
    loads = []
    for k in range(slots):
        for q in range(chunks):
            part = pl.ds(q * depth, depth)
            load = pltpu.make_async_copy(weights.at[0, 0, k, part], wbuf.at[k, part], wsem.at[k, q])
            load.start()
            loads.append(load)

    barrier = pltpu.get_barrier_semaphore()
    for step in range(1, n):
        pl.semaphore_signal(barrier, inc=1, device_id={"vox": (me + step) % n}, device_id_type=MESH)
    for load in arguments:
        load.wait()
    meta[...] = jnp.where(
        lane_iota(meta.shape) == slots, jnp.full(meta.shape, counts[0, 0]), 0
    )
    meta[0:1, 0:slots] = ids[0]
    meta[1:2, 0:slots] = offs[0]
    low = image[0].astype(jnp.bfloat16)
    flat = jnp.concatenate([low[r : r + 1] for r in range(low.shape[0])], axis=1)
    flat = jnp.broadcast_to(flat, (SB, voxels))
    mask = block_mask(SB * WIN)
    alive = jnp.full((SB, LANES), counts[0, 0])
    left = lane_iota((SB, LANES)) < WIN
    pl.semaphore_wait(barrier, n - 1)

    def remote(src, dst, send, recv, target):
        return pltpu.make_async_remote_copy(
            src_ref=src, dst_ref=dst, send_sem=send, recv_sem=recv,
            device_id={"vox": target}, device_id_type=MESH,
        )

    small, sends = [], []
    for step in range(1, n):
        copy = remote(meta, meta_all.at[me], small_send.at[step], small_recv.at[step], (me + step) % n)
        copy.start()
        small.append(copy)
    own_meta = pltpu.make_async_copy(meta, meta_all.at[me], local_sem.at[0])
    own_meta.start()
    for side, target in ((0, (me + 1) % n), (1, (me + n - 1) % n)):
        copy = remote(image.at[0], halo.at[side], halo_send.at[side], halo_recv.at[side], target)
        copy.start()
        sends.append(copy)

    locals_ = [own_meta]
    packed = None
    for k in range(slots):
        total = jnp.zeros((SB, SB * WIN), jnp.float32)
        for q in range(chunks):
            loads[k * chunks + q].wait()
            total = total + jnp.dot(
                flat[:, q * depth : (q + 1) * depth],
                wbuf[k, q * depth : (q + 1) * depth],
                preferred_element_type=jnp.float32,
            )
        total = jnp.where(mask, total, 0.0)
        tile = total[:, 0:LANES]
        for g in range(1, SB * WIN // LANES):
            tile = tile + total[:, g * LANES : (g + 1) * LANES]
        tile = tile + pltpu.roll(tile, WIN, 1)
        tile = jnp.where(alive > k, tile, 0.0)
        packed = jnp.where(left, tile, 0.0) if k % 2 == 0 else jnp.where(left, packed, tile)
        if k % 2 == 1 or k == slots - 1:
            g = k // 2
            mine[g] = packed
            for step in range(1, n):
                copy = remote(
                    mine.at[g], pieces_all.at[me, g], piece_send.at[g, step], piece_recv.at[g, step],
                    (me + step) % n,
                )
                copy.start()
                sends.append(copy)
            copy = pltpu.make_async_copy(mine.at[g], pieces_all.at[me, g], local_sem.at[1 + g])
            copy.start()
            locals_.append(copy)

    for copy in locals_:
        copy.wait()
    for copy in small + sends:
        copy.wait()


def place_kernel(
    n, slots, pieces_all, meta_all, measured,
    windows, residual, signals, adjoints, table, meta_sem,
):
    me = lax.axis_index("vox")
    rows, samples = measured.shape[1:]
    tables = pltpu.make_async_copy(meta_all, table, meta_sem)
    tables.start()
    signals[...] = jnp.zeros_like(signals)
    adjoints[:, pl.ds(samples, LANES)] = jnp.zeros((adjoints.shape[0], LANES), jnp.float32)
    if rows < SB:
        adjoints[...] = jnp.zeros_like(adjoints)
    tables.wait()
    at = lane_iota((SB, LANES))

    def place(j, carry):
        for k in range(slots):
            number = table[j, 0, k]
            start = table[j, 1, k]
            shift = start % LANES
            base = pl.multiple_of((start // LANES + 1) * LANES, LANES)
            sensors = pl.ds(pl.multiple_of(number * SB, SB), SB)
            packed = pieces_all[j, k // 2]
            keep = (at < WIN) if k % 2 == 0 else (at >= WIN)
            turn = shift if k % 2 == 0 else (shift + WIN) % LANES
            piece = pltpu.roll(jnp.where(keep, packed, 0.0), turn, 1)
            signals[sensors, pl.ds(base, LANES)] += jnp.where(at >= shift, piece, 0.0)
            after = pl.multiple_of(base + LANES, LANES)
            signals[sensors, pl.ds(after, LANES)] += jnp.where(at < shift, piece, 0.0)
        return carry

    lax.fori_loop(0, n, place, 0)

    for r in range(0, rows, 8):
        line = pl.multiple_of((me * rows + r) // 8 * 8, 8)
        block = stencil_edges(signals[pl.ds(line, 8), pl.ds(LANES, samples)])
        if rows % 8 == 0:
            block = block - measured[0, r : r + 8].astype(jnp.float32)
            residual[0, r : r + 8] = block
            block = -stencil_edges(block)
        else:
            which = jnp.full((rows, samples), (me * rows) % 8)
            part = block[0:rows]
            for i in range(1, 8 // rows):
                part = jnp.where(which == i * rows, block[i * rows : (i + 1) * rows], part)
            part = part - measured[0].astype(jnp.float32)
            residual[0] = part
            part = -stencil_edges(part)
            block = jnp.concatenate(
                [jnp.where(which == i * rows, part, 0.0) for i in range(8 // rows)], axis=0
            )
        spot = r if rows >= SB else pl.multiple_of((me * rows + r) % SB // 8 * 8, 8)
        adjoints[pl.ds(spot, 8), pl.ds(0, samples)] = block

    per = max(rows // SB, 1)
    home = me * rows // SB

    def cut(j, carry):
        packed = None
        for k in range(slots):
            number = table[j, 0, k]
            start = table[j, 1, k]
            near = number - home
            mine = (near >= 0) & (near < per) & (k < table[j, 0, slots])
            line = pl.ds(pl.multiple_of(jnp.clip(near, 0, per - 1) * SB, SB), SB)
            column = pl.multiple_of(start // LANES * LANES, LANES)
            shift = start % LANES
            turn = (LANES - shift + (k % 2) * WIN) % LANES
            first = pltpu.roll(adjoints[line, pl.ds(column, LANES)], turn, 1)
            second = pltpu.roll(
                adjoints[line, pl.ds(pl.multiple_of(column + LANES, LANES), LANES)], turn, 1
            )
            window = jnp.where(at - (k % 2) * WIN < LANES - shift, first, second)
            live = jnp.full(window.shape, mine.astype(jnp.int32))
            window = jnp.where(live > 0, window, 0.0)
            packed = window if k % 2 == 0 else jnp.where(at < WIN, packed, window)
            if k % 2 == 1 or k == slots - 1:
                windows[j, k // 2] = packed.astype(windows.dtype)
        return carry

    lax.fori_loop(0, n, cut, 0)


def variation(n, place, image, halo):
    def units(volume, step_z):
        shape = volume.shape
        row = lax.broadcasted_iota(jnp.int32, shape, 0)
        below = jnp.concatenate([volume[1:], volume[shape[0] - 1 :]], axis=0)
        step_y = below - volume
        step_x = jnp.where(lane_iota(shape) < shape[1] - 1, ahead(volume, 1) - volume, 0.0)
        size = jnp.sqrt(step_z * step_z + step_y * step_y + step_x * step_x + TV_EPS)
        return step_z / size, step_y / size, step_x / size, row

    volume = image[0]
    before, after = halo[0], halo[1]
    is_first = jnp.full(volume.shape, place) == 0
    is_last = jnp.full(volume.shape, place) == n - 1
    lower_z, _, _, _ = units(before, volume - before)
    unit_z, unit_y, unit_x, row = units(volume, jnp.where(is_last, 0.0, after - volume))
    tv = jnp.where(is_first, 0.0, lower_z) - unit_z
    shifted_y = jnp.concatenate([jnp.zeros_like(unit_y[0:1]), unit_y[: unit_y.shape[0] - 1]], axis=0)
    tv = tv + shifted_y - unit_y
    tv = tv + jnp.where(lane_iota(volume.shape) >= 1, ahead(unit_x, -1), 0.0) - unit_x
    return tv


def update_kernel(
    n, ns, windows, wbuf, image, halo, out, windows_all, grad, parts, send, recv, window_send, window_recv
):
    mine = lax.axis_index("sen")
    place = lax.axis_index("vox")
    barrier = pltpu.get_barrier_semaphore()
    for step in range(1, ns):
        pl.semaphore_signal(
            barrier, inc=1, device_id={"sen": (mine + step) % ns}, device_id_type=MESH
        )
    for step in range(1, n):
        pl.semaphore_signal(
            barrier, inc=1, device_id={"vox": (place + step) % n}, device_id_type=MESH
        )
    pl.semaphore_wait(barrier, ns + n - 2)
    exchanges = []
    for step in range(1, n):
        to = (place + step) % n
        copy = pltpu.make_async_remote_copy(
            src_ref=windows.at[to], dst_ref=windows_all.at[step - 1], send_sem=window_send.at[step],
            recv_sem=window_recv.at[step], device_id={"vox": to}, device_id_type=MESH,
        )
        copy.start()
        exchanges.append(copy)
    tv = variation(n, place, image, halo)
    for copy in exchanges:
        copy.wait()
    mask = block_mask(SB * WIN)
    left = lane_iota((SB, LANES)) < WIN
    part = None
    for g in range(windows.shape[1]):
        packed = windows[place, g].astype(jnp.float32)
        for step in range(1, n):
            packed = packed + windows_all[step - 1, g].astype(jnp.float32)
        turned = pltpu.roll(packed, WIN, 1)
        for k in range(2 * g, min(2 * g + 2, wbuf.shape[0])):
            window = jnp.where(left, packed, turned) if k % 2 == 0 else jnp.where(left, turned, packed)
            spread = jnp.concatenate([window] * (SB * WIN // LANES), axis=1)
            spread = jnp.where(mask, spread, 0.0).astype(jnp.bfloat16)
            term = lax.dot_general(
                spread, wbuf[k], (((1,), (1,)), ((), ())), preferred_element_type=jnp.float32
            )
            part = term if part is None else part + term
    grad[...] = jnp.sum(part, axis=0, keepdims=True)
    copies = []
    for step in range(1, ns):
        copy = pltpu.make_async_remote_copy(
            src_ref=grad, dst_ref=parts.at[mine], send_sem=send.at[step], recv_sem=recv.at[step],
            device_id={"sen": (mine + step) % ns}, device_id_type=MESH,
        )
        copy.start()
        copies.append(copy)

    for copy in copies:
        copy.wait()
    flat = None
    for index in range(ns):
        chosen = jnp.full(grad.shape, mine) == index
        term = jnp.where(chosen, grad[...], parts[index])
        flat = term if flat is None else flat + term
    volume = image[0]
    width = volume.shape[1]
    for r in range(volume.shape[0]):
        total = flat[:, r * width : (r + 1) * width]
        out[0, r : r + 1] = volume[r : r + 1] - STEP_SIZE * (total + TV_WEIGHT * tv[r : r + 1])


def on_device(image, weights, block_ids, offsets, counts, measured):
    n = lax.axis_size("vox")
    ns = lax.axis_size("sen")
    slots, voxels, cells = weights.shape[2:]
    rows, samples = measured.shape[1:]
    groups = (slots + 1) // 2
    chunks = 4
    vmem = pl.BlockSpec(memory_space=pltpu.VMEM)
    smem = pl.BlockSpec(memory_space=pltpu.SMEM)
    hbm = pl.BlockSpec(memory_space=pltpu.HBM)
    anywhere = pl.BlockSpec(memory_space=pl.ANY)
    dma = pltpu.SemaphoreType.DMA
    shape = jax.ShapeDtypeStruct

    def pin(value):
        return pltpu.with_memory_space_constraint(value, pltpu.HBM)

    pieces_all, meta_all, halo, held = pl.pallas_call(
        functools.partial(gather_kernel, n, slots, chunks),
        out_shape=(
            shape((n, groups, SB, LANES), jnp.float32),
            shape((n, 2, LANES), jnp.int32),
            shape((2,) + image.shape[1:], jnp.float32),
            shape((slots, voxels, cells), jnp.bfloat16),
        ),
        in_specs=[hbm, hbm, hbm, hbm, smem],
        out_specs=(vmem,) * 4,
        scratch_shapes=[
            pltpu.VMEM(image.shape, jnp.float32),
            pltpu.VMEM(block_ids.shape, jnp.int32),
            pltpu.VMEM(offsets.shape, jnp.int32),
            pltpu.VMEM((groups, SB, LANES), jnp.float32),
            pltpu.VMEM((2, LANES), jnp.int32),
            dma((slots, chunks)),
            dma((3,)),
            dma((1 + groups,)),
            dma((n,)),
            dma((n,)),
            dma((2,)),
            dma((2,)),
            dma((groups, n)),
            dma((groups, n)),
        ],
        compiler_params=pltpu.CompilerParams(
            collective_id=0, has_side_effects=True, vmem_limit_bytes=16 << 20
        ),
        name="gather_kernel",
    )(pin(image), pin(weights), pin(block_ids), pin(offsets), counts)

    windows, residual = pl.pallas_call(
        functools.partial(place_kernel, n, slots),
        out_shape=(
            shape((n, groups, SB, LANES), jnp.bfloat16),
            shape(measured.shape, jnp.float32),
        ),
        in_specs=[vmem, anywhere, vmem],
        out_specs=(vmem, vmem),
        scratch_shapes=[
            pltpu.VMEM((rows * n, samples + 3 * LANES), jnp.float32),
            pltpu.VMEM((max(rows, SB), samples + LANES), jnp.float32),
            pltpu.SMEM((n, 2, LANES), jnp.int32),
            dma,
        ],
        compiler_params=pltpu.CompilerParams(vmem_limit_bytes=16 << 20),
        name="place_kernel",
    )(pieces_all, meta_all, measured)

    image_next = pl.pallas_call(
        functools.partial(update_kernel, n, ns),
        out_shape=shape(image.shape, jnp.float32),
        in_specs=[vmem] * 4,
        out_specs=vmem,
        scratch_shapes=[
            pltpu.VMEM((n - 1, groups, SB, LANES), jnp.bfloat16),
            pltpu.VMEM((1, voxels), jnp.float32),
            pltpu.VMEM((ns, 1, voxels), jnp.float32),
            dma((ns,)),
            dma((ns,)),
            dma((n,)),
            dma((n,)),
        ],
        compiler_params=pltpu.CompilerParams(
            collective_id=1, has_side_effects=True, vmem_limit_bytes=16 << 20
        ),
        name="update_kernel",
    )(windows, held, image, halo)
    return (image_next, residual)


def solution(mesh):
    placed = (
        P("vox", None, None),
        P("vox", "sen", None, None, None),
        P("vox", "sen", None),
        P("vox", "sen", None),
        P("vox", "sen"),
        P("sen", "vox", None),
    )
    return jax.shard_map(
        on_device,
        mesh=mesh,
        in_specs=placed,
        out_specs=(P("vox", None, None), P("sen", "vox", None)),
        check_vma=False,
    )
```

profile of v0, /device:TPU:0, one launch (start us, length us, event | category | flops | bytes accessed | tf_op | source)
XLA Modules:
  0.0 31.7 jit_solution(1039299710951476255)
XLA Ops:
  0.6 0.0 copy-start.1
  0.6 0.0 copy-start
  1.3 12.7 %gather_kernel.1 = (f32[8,3,16,128]{3,2,1,0:T(8,128)S(1)}, s32[8,2,128]{2,1,0:T(2,128)S(1)}, f32[2,2,512]{2,1,0:T(2,128)S(1)}, bf16[5,1024,1024]{2,1,0:T(8,128)(2,1)S(1)}) custom-call(f32[1,2,512]{2,1,0:T(2,128)} %image.1, bf16[1,1,5,1024,1024]{4,3,2,1,0:T(8,128)(2,1)} %weights.1, s32[1,1,5]{2,1,0:T(1,128)} %ids_in.1, s32[1,1,5]{2,1,0:T(1,128)} %offs_in.1, ...), custom_call_target="tpu_custom_call" | custom-call | tf_op jit(solution)/shard_map/gather_kernel/pallas_call | solution.py:339
  14.0 0.0 copy-done
  14.1 4.0 %place_kernel.1 = (bf16[8,3,16,128]{3,2,1,0:T(8,128)(2,1)S(1)}, f32[1,32,2048]{2,1,0:T(8,128)}) custom-call(f32[8,3,16,128]{3,2,1,0:T(8,128)S(1)} %get-tuple-element.8.pieces_all, s32[8,2,128]{2,1,0:T(2,128)S(1)} %get-tuple-element.9.meta_all, bf16[1,32,2048]{2,1,0:T(8,128)(2,1)S(1)} %copy-done), custom_call_target="tpu_custom_call" | custom-call | tf_op jit(solution)/shard_map/place_kernel/pallas_call | solution.py:371
  18.1 0.0 copy-done.1
  18.1 13.0 %update_kernel.1 = f32[1,2,512]{2,1,0:T(2,128)S(1)} custom-call(bf16[8,3,16,128]{3,2,1,0:T(8,128)(2,1)S(1)} %get-tuple-element.10.windows, bf16[5,1024,1024]{2,1,0:T(8,128)(2,1)S(1)} %get-tuple-element.11.wbuf, f32[1,2,512]{2,1,0:T(2,128)S(1)} %copy-done.1, f32[2,2,512]{2,1,0:T(2,128)S(1)} %get-tuple-element.12.halo), custom_call_target="tpu_custom_call" | custom-call | tf_op jit(solution)/shard_map/update_kernel/pallas_call | solution.py:389
  31.1 0.6 %copy.10 = f32[1,2,512]{2,1,0:T(2,128)} copy(f32[1,2,512]{2,1,0:T(2,128)S(1)} %update_kernel.1) | data formatting | bytes 8192
Async XLA Ops:
  0.6 17.5 %copy-start.1 = (f32[1,2,512]{2,1,0:T(2,128)S(1)}, f32[1,2,512]{2,1,0:T(2,128)}, u32[]{:S(2)}) copy-start(f32[1,2,512]{2,1,0:T(2,128)} %image.1) | copy-start | bytes 12292
  0.6 13.4 %copy-start = (bf16[1,32,2048]{2,1,0:T(8,128)(2,1)S(1)}, bf16[1,32,2048]{2,1,0:T(8,128)(2,1)}, u32[]{:S(2)}) copy-start(bf16[1,32,2048]{2,1,0:T(8,128)(2,1)} %measured.1) | copy-start | bytes 393220
where the time goes:
time: 31.9 us; the launch traced here: 31.7 us
  Pallas kernels  29.8 us (93%)
  between operations  1.37 us (4%)
  local copies, waits for them, and re-layouts  0.6 us (2%)
    pallas_call x1, Pallas kernels, on_device(): pl.pallas_call(functools.partial(update_kernel, n, ns), out_shape=shape(i...  13 us
    pallas_call x1, Pallas kernels, on_device(): pl.pallas_call(functools.partial(gather_kernel, n, slots, chunks), out_sh...  12.7 us
    pallas_call x1, Pallas kernels, on_device(): pl.pallas_call(functools.partial(place_kernel, n, slots), out_shape=(shap...  4.04 us

commit v1 on v0

v1 whole, which is shorter than its diff:
```python
import functools

import jax
import jax.numpy as jnp
from jax import lax
from jax.experimental import pallas as pl
from jax.experimental.pallas import tpu as pltpu
from jax.sharding import PartitionSpec as P

SB = 16
WIN = 64
LANES = 128
HALF = 8
FAR = 1 << 16
UNROLL = 8

STEP_SIZE = 0.25
TV_WEIGHT = 0.3
TV_EPS = 0.01
C1 = 8.0 / 12.0
C2 = 1.0 / 12.0
MESH = pl.DeviceIdType.MESH


def lane_iota(shape):
    return lax.broadcasted_iota(jnp.int32, shape, len(shape) - 1)


def ahead(value, shift):
    length = value.shape[-1]
    return pltpu.roll(value, (-shift) % length, value.ndim - 1)


def stencil(value):
    return C2 * ahead(value, -2) - C1 * ahead(value, -1) + C1 * ahead(value, 1) - C2 * ahead(value, 2)


def stencil_edges(value):
    length = value.shape[-1]
    at = lane_iota(value.shape)
    total = jnp.where(at >= 2, C2 * ahead(value, -2), 0.0)
    total = total - jnp.where(at >= 1, C1 * ahead(value, -1), 0.0)
    total = total + jnp.where(at < length - 1, C1 * ahead(value, 1), 0.0)
    return total - jnp.where(at < length - 2, C2 * ahead(value, 2), 0.0)


def block_mask(width):
    row = lax.broadcasted_iota(jnp.int32, (SB, width), 0)
    return lane_iota((SB, width)) // WIN == row


def each(count, body, carry):
    if count > UNROLL:
        return lax.fori_loop(0, count, body, carry)
    for i in range(count):
        carry = body(i, carry)
    return carry


def gather_kernel(
    n, slots, chunks, image_in, weights, ids_in, offs_in, count, measured_in,
    turned, target, windows, halo, wbuf, image, measured,
    ids, offs, mine, meta, table, pieces_all, tiled, cuts, cuts_all,
    wsem, load_sem, local_sem, small_send, small_recv, halo_send, halo_recv,
    piece_send, piece_recv, cut_send, cut_recv,
):
    me = lax.axis_index("vox")
    voxels = weights.shape[3]
    depth = voxels // chunks
    rows, samples = measured.shape[1:]
    tiles = samples // LANES
    lines = min(rows, SB)
    parts = SB // lines
    per = max(rows // SB, 1)

    barrier = pltpu.get_barrier_semaphore()
    for step in range(1, n):
        pl.semaphore_signal(barrier, inc=1, device_id={"vox": (me + step) % n}, device_id_type=MESH)

    arguments = []
    pairs = ((ids_in, ids), (offs_in, offs), (image_in, image), (measured_in, measured))
    for i, (src, dst) in enumerate(pairs):
        load = pltpu.make_async_copy(src, dst, load_sem.at[i])
        load.start()
        arguments.append(load)
    loads = []
    for k in range(slots):
        for q in range(chunks):
            part = pl.ds(q * depth, depth)
            load = pltpu.make_async_copy(weights.at[0, 0, k, part], wbuf.at[k, part], wsem.at[k, q])
            load.start()
            loads.append(load)

    for load in arguments:
        load.wait()
    meta[...] = jnp.where(lane_iota(meta.shape) == slots, jnp.full(meta.shape, count[0, 0]), 0)
    meta[0:1, 0:slots] = ids[0]
    meta[1:2, 0:slots] = offs[0]
    for i in range(per * tiles):
        tiled[i] = measured[0, i // tiles * SB : i // tiles * SB + lines, i % tiles * LANES : (i % tiles + 1) * LANES]
    low = image[0].astype(jnp.bfloat16)
    flat = jnp.concatenate([low[r : r + 1] for r in range(low.shape[0])], axis=1)
    flat = jnp.broadcast_to(flat, (SB, voxels))
    mask = block_mask(SB * WIN)
    alive = jnp.full((SB, LANES), count[0, 0])
    left = lane_iota((SB, LANES)) < WIN
    pl.semaphore_wait(barrier, n - 1)

    def remote(src, dst, send, recv, target):
        return pltpu.make_async_remote_copy(
            src_ref=src, dst_ref=dst, send_sem=send, recv_sem=recv,
            device_id={"vox": target}, device_id_type=MESH,
        )

    small, sends, locals_ = [], [], []
    for step in range(1, n):
        copy = remote(meta, table.at[me], small_send.at[step], small_recv.at[step], (me + step) % n)
        copy.start()
        small.append(copy)
    own_meta = pltpu.make_async_copy(meta, table.at[me], local_sem.at[0])
    own_meta.start()
    for side, to in ((0, (me + 1) % n), (1, (me + n - 1) % n)):
        copy = remote(image.at[0], halo.at[side], halo_send.at[side], halo_recv.at[side], to)
        copy.start()
        sends.append(copy)

    at = lane_iota((HALF, LANES))

    def forward(k):
        total = jnp.zeros((SB, SB * WIN), jnp.float32)
        for q in range(chunks):
            loads[k * chunks + q].wait()
            total = total + jnp.dot(
                flat[:, q * depth : (q + 1) * depth],
                wbuf[k, q * depth : (q + 1) * depth],
                preferred_element_type=jnp.float32,
            )
        total = jnp.where(mask, total, 0.0)
        tile = total[:, 0:LANES]
        for g in range(1, SB * WIN // LANES):
            tile = tile + total[:, g * LANES : (g + 1) * LANES]
        tile = tile + pltpu.roll(tile, WIN, 1)
        return jnp.where(alive > k, tile, 0.0)

    def cut(j, carry):
        across = lane_iota((lines, LANES))
        for k in range(slots):
            near = jnp.clip(table[j, 0, k] - me * per, 0, per - 1) * tiles
            base = jnp.maximum(table[j, 1, k] - 2, 0)
            first = base // LANES
            after = jnp.minimum(first + 1, tiles - 1)
            edge = base % LANES
            one = tiled[near + first].astype(jnp.float32)
            two = tiled[near + after].astype(jnp.float32)
            both = jnp.where(across >= edge, one, two)
            cuts[j, k] = both.astype(cuts.dtype)
        return carry

    packed = None
    for k in range(slots):
        if k == slots - 1:
            own_meta.wait()
            for copy in small:
                copy.wait()
            each(n, cut, 0)
            exchanged = []
            for step in range(1, n):
                to = (me + step) % n
                copy = remote(cuts.at[to], cuts_all.at[me], cut_send.at[step], cut_recv.at[step], to)
                copy.start()
                exchanged.append(copy)
            copy = pltpu.make_async_copy(cuts.at[me], cuts_all.at[me], local_sem.at[1])
            copy.start()
            exchanged.append(copy)
        tile = forward(k)
        packed = jnp.where(left, tile, 0.0) if k % 2 == 0 else jnp.where(left, packed, tile)
        if k % 2 == 1 or k == slots - 1:
            g = k // 2
            mine[g] = packed
            group = []
            for step in range(1, n):
                copy = remote(
                    mine.at[g], pieces_all.at[me, g], piece_send.at[g, step], piece_recv.at[g, step],
                    (me + step) % n,
                )
                copy.start()
                group.append(copy)
            copy = pltpu.make_async_copy(mine.at[g], pieces_all.at[me, g], local_sem.at[2 + g])
            copy.start()
            group.append(copy)
            locals_.append(group)

    numbers = [table[me, 0, k] for k in range(slots)]
    starts = [table[me, 1, k] for k in range(slots)]
    times = [start - WIN // 2 + ((at - start + WIN // 2) & (LANES - 1)) for start in starts]
    keys = [number * FAR + time for number, time in zip(numbers, times)]
    lane = lane_iota((1, LANES))

    sums = [jnp.zeros((HALF, LANES), jnp.float32)] * (slots * 2)
    for g, group in enumerate(locals_):
        for copy in group:
            copy.wait()

        def gather(j, sums, g=g):
            sums = list(sums)
            packed = pieces_all[j, g]
            for k in range(2 * g, min(2 * g + 2, slots)):
                number, start = table[j, 0, k], table[j, 1, k]
                piece = pltpu.roll(packed, (start + (k % 2) * WIN) & (LANES - 1), 1)
                turned[j, k] = piece
                since = (lane - start) & (LANES - 1)
                spot = number * tiles + lax.shift_right_logical(since + start, 7)
                target[j, k : k + 1] = jnp.where(since < WIN, spot, -1)
                key = number * FAR + start
                for i in range(slots):
                    since = keys[i] - key
                    inside = (since >= 0) & (since < WIN)
                    for h in range(2):
                        part = piece[h * HALF : (h + 1) * HALF]
                        sums[2 * i + h] = sums[2 * i + h] + jnp.where(inside, part, 0.0)
            return tuple(sums)

        sums = each(n, gather, tuple(sums))

    for copy in exchanged:
        copy.wait()
    for k in range(slots):
        parts_of = [cuts_all[numbers[k] * SB // rows + i, k].astype(jnp.float32) for i in range(parts)]
        block = parts_of[0] if parts == 1 else jnp.concatenate(parts_of, axis=0)
        live = jnp.full((HALF, LANES), table[me, 0, slots]) > k
        keep = (times[k] >= 0) & (times[k] < samples) & live
        halves = []
        for h in range(2):
            rest = stencil(sums[2 * k + h]) - block[h * HALF : (h + 1) * HALF]
            halves.append(jnp.where(keep, rest, 0.0))
        whole = jnp.concatenate(halves, axis=0)
        windows[k] = pltpu.roll(whole, (LANES - starts[k]) & (LANES - 1), 1)

    for copy in sends:
        copy.wait()


def variation(n, place, image, halo):
    def units(volume, step_z):
        shape = volume.shape
        row = lax.broadcasted_iota(jnp.int32, shape, 0)
        below = jnp.concatenate([volume[1:], volume[shape[0] - 1 :]], axis=0)
        step_y = below - volume
        step_x = jnp.where(lane_iota(shape) < shape[1] - 1, ahead(volume, 1) - volume, 0.0)
        size = jnp.sqrt(step_z * step_z + step_y * step_y + step_x * step_x + TV_EPS)
        return step_z / size, step_y / size, step_x / size, row

    volume = image[0]
    before, after = halo[0], halo[1]
    is_first = jnp.full(volume.shape, place) == 0
    is_last = jnp.full(volume.shape, place) == n - 1
    lower_z, _, _, _ = units(before, volume - before)
    unit_z, unit_y, unit_x, row = units(volume, jnp.where(is_last, 0.0, after - volume))
    tv = jnp.where(is_first, 0.0, lower_z) - unit_z
    shifted_y = jnp.concatenate([jnp.zeros_like(unit_y[0:1]), unit_y[: unit_y.shape[0] - 1]], axis=0)
    tv = tv + shifted_y - unit_y
    tv = tv + jnp.where(lane_iota(volume.shape) >= 1, ahead(unit_x, -1), 0.0) - unit_x
    return tv


def update_kernel(
    n, ns, windows, wbuf, image, halo, turned, target, measured,
    out, residual, signals, grad, parts, send, recv
):
    mine = lax.axis_index("sen")
    place = lax.axis_index("vox")
    slots = wbuf.shape[0]
    rows, samples = measured.shape[1:]
    tiles = samples // LANES
    per = max(rows // SB, 1)
    barrier = pltpu.get_barrier_semaphore()
    for step in range(1, ns):
        pl.semaphore_signal(
            barrier, inc=1, device_id={"sen": (mine + step) % ns}, device_id_type=MESH
        )
    mask = block_mask(SB * WIN)
    left = lane_iota((SB, LANES)) < WIN
    part = None
    for k in range(slots):
        window = -stencil(windows[k])
        window = jnp.where(left, window, pltpu.roll(window, WIN, 1))
        spread = jnp.concatenate([window] * (SB * WIN // LANES), axis=1)
        spread = jnp.where(mask, spread, 0.0).astype(jnp.bfloat16)
        term = lax.dot_general(
            spread, wbuf[k], (((1,), (1,)), ((), ())), preferred_element_type=jnp.float32
        )
        part = term if part is None else part + term
    grad[...] = jnp.sum(part, axis=0, keepdims=True)
    pl.semaphore_wait(barrier, ns - 1)
    copies = []
    for step in range(1, ns):
        copy = pltpu.make_async_remote_copy(
            src_ref=grad, dst_ref=parts.at[mine], send_sem=send.at[step], recv_sem=recv.at[step],
            device_id={"sen": (mine + step) % ns}, device_id_type=MESH,
        )
        copy.start()
        copies.append(copy)

    home = place * rows // SB * tiles

    def fill(i, carry):
        wanted = home + i

        def add(j, sums):
            low, high = sums
            for k in range(slots):
                here = jnp.broadcast_to(target[j, k : k + 1], (HALF, LANES)) == wanted
                low = low + jnp.where(here, turned[j, k, 0:HALF], 0.0)
                high = high + jnp.where(here, turned[j, k, HALF:SB], 0.0)
            return low, high

        low, high = each(n, add, (jnp.zeros((HALF, LANES), jnp.float32),) * 2)
        line = i // tiles * SB
        column = pl.ds(pl.multiple_of(i % tiles * LANES, LANES), LANES)
        signals[pl.ds(pl.multiple_of(line, SB), HALF), column] = low
        signals[pl.ds(pl.multiple_of(line + HALF, HALF), HALF), column] = high
        return carry

    lax.fori_loop(0, per * tiles, fill, 0)

    for r in range(0, rows, HALF):
        line = r if rows >= SB else pl.multiple_of((place * rows + r) % SB // HALF * HALF, HALF)
        block = stencil_edges(signals[pl.ds(line, HALF)])
        if rows % HALF == 0:
            residual[0, r : r + HALF] = block - measured[0, r : r + HALF].astype(jnp.float32)
        else:
            which = jnp.full((rows, samples), (place * rows) % HALF)
            own = block[0:rows]
            for i in range(1, HALF // rows):
                own = jnp.where(which == i * rows, block[i * rows : (i + 1) * rows], own)
            residual[0] = own - measured[0].astype(jnp.float32)

    tv = variation(n, place, image, halo)
    for copy in copies:
        copy.wait()
    flat = None
    for index in range(ns):
        chosen = jnp.full(grad.shape, mine) == index
        term = jnp.where(chosen, grad[...], parts[index])
        flat = term if flat is None else flat + term
    volume = image[0]
    width = volume.shape[1]
    for r in range(volume.shape[0]):
        total = flat[:, r * width : (r + 1) * width]
        out[0, r : r + 1] = volume[r : r + 1] - STEP_SIZE * (total + TV_WEIGHT * tv[r : r + 1])


def store_kernel(image, residual, image_out, residual_out, sem):
    copies = []
    for i, (src, dst) in enumerate(((residual, residual_out), (image, image_out))):
        copy = pltpu.make_async_copy(src, dst, sem.at[i])
        copy.start()
        copies.append(copy)
    for copy in copies:
        copy.wait()


def on_device(image, weights, block_ids, offsets, counts, measured):
    n = lax.axis_size("vox")
    ns = lax.axis_size("sen")
    slots, voxels, cells = weights.shape[2:]
    rows, samples = measured.shape[1:]
    groups = (slots + 1) // 2
    chunks = 4
    vmem = pl.BlockSpec(memory_space=pltpu.VMEM)
    hbm = pl.BlockSpec(memory_space=pltpu.HBM)
    smem = pl.BlockSpec(memory_space=pltpu.SMEM)
    dma = pltpu.SemaphoreType.DMA
    shape = jax.ShapeDtypeStruct

    def pin(value):
        return pltpu.with_memory_space_constraint(value, pltpu.HBM)

    turned, target, windows, halo, held, image_held, measured_held = pl.pallas_call(
        functools.partial(gather_kernel, n, slots, chunks),
        out_shape=(
            shape((n, slots, SB, LANES), jnp.float32),
            shape((n, HALF, LANES), jnp.int32),
            shape((slots, SB, LANES), jnp.float32),
            shape((2,) + image.shape[1:], jnp.float32),
            shape((slots, voxels, cells), jnp.bfloat16),
            shape(image.shape, jnp.float32),
            shape(measured.shape, measured.dtype),
        ),
        in_specs=[hbm] * 4 + [smem, hbm],
        out_specs=(vmem,) * 7,
        scratch_shapes=[
            pltpu.VMEM(block_ids.shape, jnp.int32),
            pltpu.VMEM(offsets.shape, jnp.int32),
            pltpu.VMEM((groups, SB, LANES), jnp.float32),
            pltpu.VMEM((2, LANES), jnp.int32),
            pltpu.SMEM((n, 2, LANES), jnp.int32),
            pltpu.VMEM((n, groups, SB, LANES), jnp.float32),
            pltpu.VMEM((max(rows // SB, 1) * (samples // LANES), min(rows, SB), LANES), jnp.bfloat16),
            pltpu.VMEM((n, slots, min(rows, SB), LANES), jnp.bfloat16),
            pltpu.VMEM((n, slots, min(rows, SB), LANES), jnp.bfloat16),
            dma((slots, chunks)),
            dma((4,)),
            dma((2 + groups,)),
            dma((n,)),
            dma((n,)),
            dma((2,)),
            dma((2,)),
            dma((groups, n)),
            dma((groups, n)),
            dma((n,)),
            dma((n,)),
        ],
        compiler_params=pltpu.CompilerParams(
            collective_id=0, has_side_effects=True, vmem_limit_bytes=20 << 20
        ),
        name="gather_kernel",
    )(pin(image), pin(weights), pin(block_ids), pin(offsets), counts, pin(measured))

    image_next, residual = pl.pallas_call(
        functools.partial(update_kernel, n, ns),
        out_shape=(shape(image.shape, jnp.float32), shape(measured.shape, jnp.float32)),
        in_specs=[vmem] * 7,
        out_specs=(vmem, vmem),
        scratch_shapes=[
            pltpu.VMEM((max(rows, SB), samples), jnp.float32),
            pltpu.VMEM((1, voxels), jnp.float32),
            pltpu.VMEM((ns, 1, voxels), jnp.float32),
            dma((ns,)),
            dma((ns,)),
        ],
        compiler_params=pltpu.CompilerParams(
            collective_id=1, has_side_effects=True, vmem_limit_bytes=16 << 20
        ),
        name="update_kernel",
    )(windows, held, image_held, halo, turned, target, measured_held)

    return pl.pallas_call(
        store_kernel,
        out_shape=(shape(image.shape, jnp.float32), shape(measured.shape, jnp.float32)),
        in_specs=[vmem, vmem],
        out_specs=(hbm, hbm),
        scratch_shapes=[dma((2,))],
        compiler_params=pltpu.CompilerParams(vmem_limit_bytes=1 << 20),
        name="store_kernel",
    )(image_next, residual)


def solution(mesh):
    placed = (
        P("vox", None, None),
        P("vox", "sen", None, None, None),
        P("vox", "sen", None),
        P("vox", "sen", None),
        P("vox", "sen"),
        P("sen", "vox", None),
    )
    return jax.shard_map(
        on_device,
        mesh=mesh,
        in_specs=placed,
        out_specs=(P("vox", None, None), P("sen", "vox", None)),
        check_vma=False,
    )
```

time: 31.9 us -> 25.7 us (0.81)
  Pallas kernels: 29.8 us -> 24.3 us
  local copies, waits for them, and re-layouts: 0.6 us -> 0 us
    pallas_call x2, Pallas kernels: 17 us -> 8.98 us  [the longest x1 8.26 us: on_device(): pl.pallas_call(functools.partial(update_kernel, n, ns), out_shape=(shape(...]
    pallas_call x1, Pallas kernels: 12.7 us -> 15.3 us  [on_device(): pl.pallas_call(functools.partial(gather_kernel, n, slots, chunks), out_sh...]
    unnamed x5 -> x0, local copies, waits for them, and re-layouts: 0.6 us -> none
where the time goes in v1:
time: 25.7 us; the launch traced here: 25.6 us
  Pallas kernels  24.3 us (95%)
  between operations  1.29 us (5%)
    pallas_call x1, Pallas kernels, on_device(): pl.pallas_call(functools.partial(gather_kernel, n, slots, chunks), out_sh...  15.3 us
    pallas_call x1, Pallas kernels, on_device(): pl.pallas_call(functools.partial(update_kernel, n, ns), out_shape=(shape(...  8.26 us
    pallas_call x1, Pallas kernels, on_device(): pl.pallas_call(store_kernel, out_shape=(shape(image.shape, jnp.float32),...  0.72 us

profile of v1, /device:TPU:0, one launch (start us, length us, event | category | flops | bytes accessed | tf_op | source)
XLA Modules:
  0.0 25.6 jit_solution(6218485813926215533)
XLA Ops:
  1.3 15.3 %gather_kernel.1 = (f32[8,5,16,128]{3,2,1,0:T(8,128)S(1)}, s32[8,8,128]{2,1,0:T(8,128)S(1)}, f32[5,16,128]{2,1,0:T(8,128)S(1)}, f32[2,2,512]{2,1,0:T(2,128)S(1)}...) custom-call(f32[1,2,512]{2,1,0:T(2,128)} %image_in.1, ...), custom_call_target="tpu_custom_call" | custom-call | tf_op jit(solution)/shard_map/gather_kernel/pallas_call | solution.py:379
  16.6 8.3 %update_kernel.1 = (f32[1,2,512]{2,1,0:T(2,128)S(1)}, f32[1,32,2048]{2,1,0:T(8,128)S(1)}) custom-call(f32[5,16,128]{2,1,0:T(8,128)S(1)} %get-tuple-element.11.windows, bf16[5,1024,1024]{2,1,0:T(8,128)(2,1)S(1)} %get-tuple-element.12.wbuf, f32[1,2,512]{2,1,0:T(2,128)S(1)} %get-tuple-element.13.image, f32[2,2,512]{2,1,0:T(2,128)S(1)} %get-tuple-element.14.halo, ...), custom_call_target="tpu_custom_call" | custom-call | tf_op jit(solution)/shard_map/update_kernel/pallas_call | solution.py:420
  24.8 0.7 %store_kernel.1 = (f32[1,2,512]{2,1,0:T(2,128)}, f32[1,32,2048]{2,1,0:T(8,128)}) custom-call(f32[1,2,512]{2,1,0:T(2,128)S(1)} %get-tuple-element.18.image, f32[1,32,2048]{2,1,0:T(8,128)S(1)} %get-tuple-element.19.residual), custom_call_target="tpu_custom_call" | custom-call | tf_op jit(solution)/shard_map/store_kernel/pallas_call | solution.py:438

commit v2 on v1

v2 whole, which is shorter than its diff:
```python
import functools

import jax
import jax.numpy as jnp
from jax import lax
from jax.experimental import pallas as pl
from jax.experimental.pallas import tpu as pltpu
from jax.sharding import PartitionSpec as P

SB = 16
WIN = 64
LANES = 128
HALF = 8
FAR = 1 << 16
UNROLL = 8

STEP_SIZE = 0.25
TV_WEIGHT = 0.3
TV_EPS = 0.01
C1 = 8.0 / 12.0
C2 = 1.0 / 12.0
MESH = pl.DeviceIdType.MESH


def lane_iota(shape):
    return lax.broadcasted_iota(jnp.int32, shape, len(shape) - 1)


def ahead(value, shift):
    length = value.shape[-1]
    return pltpu.roll(value, (-shift) % length, value.ndim - 1)


def stencil(value):
    return C2 * ahead(value, -2) - C1 * ahead(value, -1) + C1 * ahead(value, 1) - C2 * ahead(value, 2)


def stencil_edges(value):
    length = value.shape[-1]
    at = lane_iota(value.shape)
    total = jnp.where(at >= 2, C2 * ahead(value, -2), 0.0)
    total = total - jnp.where(at >= 1, C1 * ahead(value, -1), 0.0)
    total = total + jnp.where(at < length - 1, C1 * ahead(value, 1), 0.0)
    return total - jnp.where(at < length - 2, C2 * ahead(value, 2), 0.0)


def block_mask(width):
    row = lax.broadcasted_iota(jnp.int32, (SB, width), 0)
    return lane_iota((SB, width)) // WIN == row


def each(count, body, carry):
    if count > UNROLL:
        return lax.fori_loop(0, count, body, carry)
    for i in range(count):
        carry = body(i, carry)
    return carry


def variation(n, place, image, halo):
    def units(volume, step_z):
        shape = volume.shape
        row = lax.broadcasted_iota(jnp.int32, shape, 0)
        below = jnp.concatenate([volume[1:], volume[shape[0] - 1 :]], axis=0)
        step_y = below - volume
        step_x = jnp.where(lane_iota(shape) < shape[1] - 1, ahead(volume, 1) - volume, 0.0)
        size = jnp.sqrt(step_z * step_z + step_y * step_y + step_x * step_x + TV_EPS)
        return step_z / size, step_y / size, step_x / size, row

    volume = image[0]
    before, after = halo[0], halo[1]
    is_first = jnp.full(volume.shape, place) == 0
    is_last = jnp.full(volume.shape, place) == n - 1
    lower_z, _, _, _ = units(before, volume - before)
    unit_z, unit_y, unit_x, row = units(volume, jnp.where(is_last, 0.0, after - volume))
    tv = jnp.where(is_first, 0.0, lower_z) - unit_z
    shifted_y = jnp.concatenate([jnp.zeros_like(unit_y[0:1]), unit_y[: unit_y.shape[0] - 1]], axis=0)
    tv = tv + shifted_y - unit_y
    tv = tv + jnp.where(lane_iota(volume.shape) >= 1, ahead(unit_x, -1), 0.0) - unit_x
    return tv


def settle(ref, sem):
    pltpu.make_async_copy(ref, ref, sem).wait()


def step_kernel(
    n, ns, slots, chunks, image_in, weights, ids_in, offs_in, count, measured_in,
    out, residual,
    wbuf, turned_w, image, measured, tiled, ids, offs, meta, table, halo, mine, pieces_all,
    cuts, cuts_all, turned, target, signals, grad, parts,
    wsem, load_sem, meta_send, meta_recv, halo_send, halo_recv, piece_send, piece_recv,
    cut_send, cut_recv, grad_send, grad_recv,
):
    me = lax.axis_index("vox")
    layer = lax.axis_index("sen")
    voxels = weights.shape[3]
    depth = voxels // chunks
    rows, samples = measured.shape[1:]
    tiles = samples // LANES
    lines = min(rows, SB)
    strips = SB // lines
    per = max(rows // SB, 1)

    barrier = pltpu.get_barrier_semaphore()
    for step in range(1, n):
        pl.semaphore_signal(barrier, inc=1, device_id={"vox": (me + step) % n}, device_id_type=MESH)
    for step in range(1, ns):
        pl.semaphore_signal(barrier, inc=1, device_id={"sen": (layer + step) % ns}, device_id_type=MESH)

    arguments = []
    pairs = ((ids_in, ids), (offs_in, offs), (image_in, image), (measured_in, measured))
    for i, (src, dst) in enumerate(pairs):
        load = pltpu.make_async_copy(src, dst, load_sem.at[i])
        load.start()
        arguments.append(load)
    loads = []
    for k in range(slots):
        for q in range(chunks):
            part = pl.ds(q * depth, depth)
            load = pltpu.make_async_copy(weights.at[0, 0, k, part], wbuf.at[k, part], wsem.at[k, q])
            load.start(priority=1)
            loads.append(load)

    mask = block_mask(SB * WIN)
    alive = jnp.full((SB, LANES), count[0, 0])
    left = lane_iota((SB, LANES)) < WIN
    at = lane_iota((HALF, LANES))
    meta[...] = jnp.zeros_like(meta)
    arguments[0].wait()
    arguments[1].wait()
    meta[0:1, 0:slots] = ids[0]
    meta[1:2, 0:slots] = offs[0]
    pl.semaphore_wait(barrier, n - 1 + ns - 1)

    def remote(src, dst, send, recv, axis, to):
        pltpu.make_async_remote_copy(
            src_ref=src, dst_ref=dst, send_sem=send, recv_sem=recv,
            device_id={axis: to}, device_id_type=MESH,
        ).start()

    for step in range(1, n):
        remote(meta, table.at[me], meta_send, meta_recv, "vox", (me + step) % n)
    pltpu.make_async_copy(meta, table.at[me], meta_recv).start()
    arguments[2].wait()
    for side, to in ((0, (me + 1) % n), (1, (me + n - 1) % n)):
        remote(image.at[0], halo.at[side], halo_send, halo_recv.at[side], "vox", to)
    low = image[0].astype(jnp.bfloat16)
    flat = jnp.concatenate([low[r : r + 1] for r in range(low.shape[0])], axis=1)
    flat = jnp.broadcast_to(flat, (SB, voxels))
    arguments[3].wait()
    for i in range(per * tiles):
        tiled[i] = measured[0, i // tiles * SB : i // tiles * SB + lines, i % tiles * LANES : (i % tiles + 1) * LANES]

    def forward(k):
        total = jnp.zeros((SB, SB * WIN), jnp.float32)
        for q in range(chunks):
            loads[k * chunks + q].wait()
            total = total + jnp.dot(
                flat[:, q * depth : (q + 1) * depth],
                wbuf[k, q * depth : (q + 1) * depth],
                preferred_element_type=jnp.float32,
            )
        total = jnp.where(mask, total, 0.0)
        tile = total[:, 0:LANES]
        for g in range(1, SB * WIN // LANES):
            tile = tile + total[:, g * LANES : (g + 1) * LANES]
        tile = tile + pltpu.roll(tile, WIN, 1)
        return jnp.where(alive > k, tile, 0.0)

    packed = None
    for k in range(slots):
        tile = forward(k)
        packed = jnp.where(left, tile, 0.0) if k % 2 == 0 else jnp.where(left, packed, tile)
        if k % 2 == 1 or k == slots - 1:
            g = k // 2
            mine[g] = packed
            for step in range(1, n):
                remote(mine.at[g], pieces_all.at[g, me], piece_send, piece_recv.at[g], "vox", (me + step) % n)
            pltpu.make_async_copy(mine.at[g], pieces_all.at[g, me], piece_recv.at[g]).start()

    settle(table, meta_recv)

    def cut(j):
        across = lane_iota((lines, LANES))
        for k in range(slots):
            near = jnp.clip(table[j, 0, k] - me * per, 0, per - 1) * tiles
            base = jnp.maximum(table[j, 1, k] - 2, 0)
            first = base // LANES
            after = jnp.minimum(first + 1, tiles - 1)
            one = tiled[near + first].astype(jnp.float32)
            two = tiled[near + after].astype(jnp.float32)
            cuts[j, k] = jnp.where(across >= base % LANES, one, two).astype(cuts.dtype)

    for step in range(n - 1, 0, -1):
        to = (me + step) % n
        cut(to)
        remote(cuts.at[to], cuts_all.at[me], cut_send, cut_recv, "vox", to)
    cut(me)
    pltpu.make_async_copy(cuts.at[me], cuts_all.at[me], cut_recv).start()

    for k in range(slots):
        turned_w[k] = wbuf[k].T

    numbers = [table[me, 0, k] for k in range(slots)]
    starts = [table[me, 1, k] for k in range(slots)]
    times = [start - WIN // 2 + ((at - start + WIN // 2) & (LANES - 1)) for start in starts]
    keys = [number * FAR + time for number, time in zip(numbers, times)]
    lane = lane_iota((1, LANES))

    sums = (jnp.zeros((HALF, LANES), jnp.float32),) * (slots * 2)
    for g in range(pieces_all.shape[0]):
        settle(pieces_all.at[g], piece_recv.at[g])

        def gather(j, sums, g=g):
            sums = list(sums)
            packed = pieces_all[g, j]
            for k in range(2 * g, min(2 * g + 2, slots)):
                number, start = table[j, 0, k], table[j, 1, k]
                piece = pltpu.roll(packed, (start + (k % 2) * WIN) & (LANES - 1), 1)
                turned[j, k] = piece
                since = (lane - start) & (LANES - 1)
                spot = number * tiles + lax.shift_right_logical(since + start, 7)
                target[j, k : k + 1] = jnp.where(since < WIN, spot, -1)
                key = number * FAR + start
                for i in range(slots):
                    since = keys[i] - key
                    inside = (since >= 0) & (since < WIN)
                    for h in range(2):
                        part = piece[h * HALF : (h + 1) * HALF]
                        sums[2 * i + h] = sums[2 * i + h] + jnp.where(inside, part, 0.0)
            return tuple(sums)

        sums = each(n, gather, sums)

    derived = [stencil(value) for value in sums]
    settle(cuts_all, cut_recv)
    spreads = []
    for k in range(slots):
        stripes = [cuts_all[numbers[k] * SB // rows + i, k].astype(jnp.float32) for i in range(strips)]
        block = stripes[0] if strips == 1 else jnp.concatenate(stripes, axis=0)
        keep = (times[k] >= 0) & (times[k] < samples) & (jnp.full((HALF, LANES), count[0, 0]) > k)
        halves = []
        for h in range(2):
            rest = jnp.where(keep, derived[2 * k + h] - block[h * HALF : (h + 1) * HALF], 0.0)
            halves.append(-stencil(rest))
        window = jnp.concatenate(halves, axis=0)
        even = pltpu.roll(window, (LANES - starts[k]) & (LANES - 1), 1)
        odd = pltpu.roll(window, (LANES + WIN - starts[k]) & (LANES - 1), 1)
        window = jnp.where(left, even, odd)
        spread = jnp.concatenate([window] * (SB * WIN // LANES), axis=1)
        spreads.append(jnp.where(mask, spread, 0.0).astype(jnp.bfloat16))
    part = None
    for k in range(slots):
        term = jnp.dot(spreads[k], turned_w[k], preferred_element_type=jnp.float32)
        part = term if part is None else part + term
    grad[...] = jnp.sum(part, axis=0, keepdims=True)
    for step in range(ns - 1, 0, -1):
        remote(grad, parts.at[layer], grad_send, grad_recv, "sen", (layer + step) % ns)
    pltpu.make_async_copy(grad, parts.at[layer], grad_recv).start()

    home = me * rows // SB * tiles

    def fill(i, carry):
        wanted = home + i

        def add(j, sums):
            low, high = sums
            for k in range(slots):
                here = jnp.broadcast_to(target[j, k : k + 1], (HALF, LANES)) == wanted
                low = low + jnp.where(here, turned[j, k, 0:HALF], 0.0)
                high = high + jnp.where(here, turned[j, k, HALF:SB], 0.0)
            return low, high

        low, high = each(n, add, (jnp.zeros((HALF, LANES), jnp.float32),) * 2)
        line = i // tiles * SB
        column = pl.ds(pl.multiple_of(i % tiles * LANES, LANES), LANES)
        signals[pl.ds(pl.multiple_of(line, SB), HALF), column] = low
        signals[pl.ds(pl.multiple_of(line + HALF, HALF), HALF), column] = high
        return carry

    lax.fori_loop(0, per * tiles, fill, 0)

    for r in range(0, rows, HALF):
        line = r if rows >= SB else pl.multiple_of((me * rows + r) % SB // HALF * HALF, HALF)
        block = stencil_edges(signals[pl.ds(line, HALF)])
        if rows % HALF == 0:
            residual[0, r : r + HALF] = block - measured[0, r : r + HALF].astype(jnp.float32)
        else:
            which = jnp.full((rows, samples), (me * rows) % HALF)
            own = block[0:rows]
            for i in range(1, HALF // rows):
                own = jnp.where(which == i * rows, block[i * rows : (i + 1) * rows], own)
            residual[0] = own - measured[0].astype(jnp.float32)

    settle(halo.at[0], halo_recv.at[0])
    settle(halo.at[1], halo_recv.at[1])
    tv = variation(n, me, image, halo)
    settle(table.at[pl.ds(0, n - 1)], meta_send)
    settle(halo, halo_send)
    settle(pieces_all.at[:, pl.ds(0, n - 1)], piece_send)
    settle(cuts_all.at[pl.ds(0, n - 1)], cut_send)
    settle(parts, grad_recv)
    flat = parts[0]
    for index in range(1, ns):
        flat = flat + parts[index]
    volume = image[0]
    width = volume.shape[1]
    for r in range(volume.shape[0]):
        total = flat[:, r * width : (r + 1) * width]
        out[0, r : r + 1] = volume[r : r + 1] - STEP_SIZE * (total + TV_WEIGHT * tv[r : r + 1])
    settle(parts.at[pl.ds(0, ns - 1)], grad_send)


def store_kernel(image, residual, image_out, residual_out, sem):
    copies = []
    for i, (src, dst) in enumerate(((residual, residual_out), (image, image_out))):
        copy = pltpu.make_async_copy(src, dst, sem.at[i])
        copy.start()
        copies.append(copy)
    for copy in copies:
        copy.wait()


def on_device(image, weights, block_ids, offsets, counts, measured):
    n = lax.axis_size("vox")
    ns = lax.axis_size("sen")
    slots, voxels, cells = weights.shape[2:]
    rows, samples = measured.shape[1:]
    groups = (slots + 1) // 2
    lines = min(rows, SB)
    chunks = 4
    vmem = pl.BlockSpec(memory_space=pltpu.VMEM)
    hbm = pl.BlockSpec(memory_space=pltpu.HBM)
    smem = pl.BlockSpec(memory_space=pltpu.SMEM)
    dma = pltpu.SemaphoreType.DMA
    shape = jax.ShapeDtypeStruct

    def pin(value):
        return pltpu.with_memory_space_constraint(value, pltpu.HBM)

    image_next, residual = pl.pallas_call(
        functools.partial(step_kernel, n, ns, slots, chunks),
        out_shape=(shape(image.shape, jnp.float32), shape(measured.shape, jnp.float32)),
        in_specs=[hbm] * 4 + [smem, hbm],
        out_specs=(vmem, vmem),
        scratch_shapes=[
            pltpu.VMEM((slots, voxels, cells), jnp.bfloat16),
            pltpu.VMEM((slots, cells, voxels), jnp.bfloat16),
            pltpu.VMEM(image.shape, jnp.float32),
            pltpu.VMEM(measured.shape, measured.dtype),
            pltpu.VMEM((max(rows // SB, 1) * (samples // LANES), lines, LANES), jnp.bfloat16),
            pltpu.VMEM(block_ids.shape, jnp.int32),
            pltpu.VMEM(offsets.shape, jnp.int32),
            pltpu.VMEM((2, LANES), jnp.int32),
            pltpu.SMEM((n, 2, LANES), jnp.int32),
            pltpu.VMEM((2,) + image.shape[1:], jnp.float32),
            pltpu.VMEM((groups, SB, LANES), jnp.float32),
            pltpu.VMEM((groups, n, SB, LANES), jnp.float32),
            pltpu.VMEM((n, slots, lines, LANES), jnp.bfloat16),
            pltpu.VMEM((n, slots, lines, LANES), jnp.bfloat16),
            pltpu.VMEM((n, slots, SB, LANES), jnp.float32),
            pltpu.VMEM((n, HALF, LANES), jnp.int32),
            pltpu.VMEM((max(rows, SB), samples), jnp.float32),
            pltpu.VMEM((1, voxels), jnp.float32),
            pltpu.VMEM((ns, 1, voxels), jnp.float32),
            dma((slots, chunks)),
            dma((4,)),
            dma,
            dma,
            dma,
            dma((2,)),
            dma,
            dma((groups,)),
            dma,
            dma,
            dma,
            dma,
        ],
        compiler_params=pltpu.CompilerParams(
            collective_id=0, has_side_effects=True, vmem_limit_bytes=40 << 20
        ),
        name="step_kernel",
    )(pin(image), pin(weights), pin(block_ids), pin(offsets), counts, pin(measured))

    return pl.pallas_call(
        store_kernel,
        out_shape=(shape(image.shape, jnp.float32), shape(measured.shape, jnp.float32)),
        in_specs=[vmem, vmem],
        out_specs=(hbm, hbm),
        scratch_shapes=[dma((2,))],
        compiler_params=pltpu.CompilerParams(vmem_limit_bytes=1 << 20),
        name="store_kernel",
    )(image_next, residual)


def solution(mesh):
    placed = (
        P("vox", None, None),
        P("vox", "sen", None, None, None),
        P("vox", "sen", None),
        P("vox", "sen", None),
        P("vox", "sen"),
        P("sen", "vox", None),
    )
    return jax.shard_map(
        on_device,
        mesh=mesh,
        in_specs=placed,
        out_specs=(P("vox", None, None), P("sen", "vox", None)),
        check_vma=False,
    )
```

time: 25.7 us -> 21.3 us (0.83)
  Pallas kernels: 24.3 us -> 19.8 us
    pallas_call x2 -> x1, Pallas kernels: 23.5 us -> 19.1 us  [on_device(): pl.pallas_call(functools.partial(step_kernel, n, ns, slots, chunks), out_...]
where the time goes in v2:
time: 21.3 us; the launch traced here: 21.1 us
  Pallas kernels  19.8 us (93%)
  between operations  1.29 us (6%)
    pallas_call x1, Pallas kernels, on_device(): pl.pallas_call(functools.partial(step_kernel, n, ns, slots, chunks), out_...  19.1 us
    pallas_call x1, Pallas kernels, on_device(): pl.pallas_call(store_kernel, out_shape=(shape(image.shape, jnp.float32),...  0.72 us

profile of v2, /device:TPU:0, one launch (start us, length us, event | category | flops | bytes accessed | tf_op | source)
XLA Modules:
  0.0 21.1 jit_solution(9000653415322282515)
XLA Ops:
  1.3 19.1 %step_kernel.1 = (f32[1,2,512]{2,1,0:T(2,128)S(1)}, f32[1,32,2048]{2,1,0:T(8,128)S(1)}) custom-call(f32[1,2,512]{2,1,0:T(2,128)} %image_in.1, bf16[1,1,5,1024,1024]{4,3,2,1,0:T(8,128)(2,1)} %weights.1, s32[1,1,5]{2,1,0:T(1,128)} %ids_in.1, s32[1,1,5]{2,1,0:T(1,128)} %offs_in.1, s32[1,1]{1,0:T(1,128)S(6)} %copy.8.count, bf16[1,32,2048]{2,1,0:T(8,128)(2,1)} %measured_in.1), custom_call_target="tpu_custom_call" | custom-call | tf_op jit(solution)/shard_map/step_kernel/pallas_call | solution.py:342
  20.4 0.7 %store_kernel.1 = (f32[1,2,512]{2,1,0:T(2,128)}, f32[1,32,2048]{2,1,0:T(8,128)}) custom-call(f32[1,2,512]{2,1,0:T(2,128)S(1)} %get-tuple-element.4.image, f32[1,32,2048]{2,1,0:T(8,128)S(1)} %get-tuple-element.5.residual), custom_call_target="tpu_custom_call" | custom-call | tf_op jit(solution)/shard_map/store_kernel/pallas_call | solution.py:386

commit v3 on v2

--- a/solution.py
+++ b/solution.py
@@ -11,6 +11,8 @@
 WIN = 64
 LANES = 128
 HALF = 8
+EDGE = 2
+SPAN = WIN + 2 * EDGE
 FAR = 1 << 16
 UNROLL = 8
 
@@ -47,6 +49,10 @@
 def block_mask(width):
     row = lax.broadcasted_iota(jnp.int32, (SB, width), 0)
     return lane_iota((SB, width)) // WIN == row
+
+
+def peer(me, count, step):
+    return me ^ step if count & (count - 1) == 0 else (me + step) % count
 
 
 def each(count, body, carry):
@@ -87,9 +93,9 @@
 def step_kernel(
     n, ns, slots, chunks, image_in, weights, ids_in, offs_in, count, measured_in,
     out, residual,
-    wbuf, turned_w, image, measured, tiled, ids, offs, meta, table, halo, mine, pieces_all,
+    wbuf, turned_w, image, measured, tiled, ids, offs, meta, table, halo, mine, pieces_all, lone, lone_all,
     cuts, cuts_all, turned, target, signals, grad, parts,
-    wsem, load_sem, meta_send, meta_recv, halo_send, halo_recv, piece_send, piece_recv,
+    wsem, load_sem, meta_send, meta_recv, halo_send, halo_recv, piece_send, piece_recv, lone_recv,
     cut_send, cut_recv, grad_send, grad_recv,
 ):
     me = lax.axis_index("vox")
@@ -140,7 +146,7 @@
         ).start()
 
     for step in range(1, n):
-        remote(meta, table.at[me], meta_send, meta_recv, "vox", (me + step) % n)
+        remote(meta, table.at[me], meta_send, meta_recv, "vox", peer(me, n, n - step))
     pltpu.make_async_copy(meta, table.at[me], meta_recv).start()
     arguments[2].wait()
     for side, to in ((0, (me + 1) % n), (1, (me + n - 1) % n)):
@@ -168,34 +174,52 @@
         tile = tile + pltpu.roll(tile, WIN, 1)
         return jnp.where(alive > k, tile, 0.0)
 
-    packed = None
+    def spread_out(src, dst, recv):
+        for step in range(1, n):
+            remote(src, dst, piece_send, recv, "vox", peer(me, n, n - step))
+        pltpu.make_async_copy(src, dst, recv).start()
+
+    first = None
     for k in range(slots):
         tile = forward(k)
-        packed = jnp.where(left, tile, 0.0) if k % 2 == 0 else jnp.where(left, packed, tile)
-        if k % 2 == 1 or k == slots - 1:
-            g = k // 2
-            mine[g] = packed
-            for step in range(1, n):
-                remote(mine.at[g], pieces_all.at[g, me], piece_send, piece_recv.at[g], "vox", (me + step) % n)
-            pltpu.make_async_copy(mine.at[g], pieces_all.at[g, me], piece_recv.at[g]).start()
+        if k % 2 == 1:
+            mine[k // 2] = jnp.where(left, first, tile)
+            spread_out(mine.at[k // 2], pieces_all.at[k // 2, me], piece_recv.at[k // 2])
+        elif k == slots - 1:
+            lone[...] = jnp.where(left[0:HALF], tile[0:HALF], tile[HALF:SB])
+            spread_out(lone, lone_all.at[me], lone_recv)
+        first = tile
 
     settle(table, meta_recv)
 
     def cut(j):
         across = lane_iota((lines, LANES))
+        spans = []
         for k in range(slots):
             near = jnp.clip(table[j, 0, k] - me * per, 0, per - 1) * tiles
-            base = jnp.maximum(table[j, 1, k] - 2, 0)
+            start = table[j, 1, k]
+            base = jnp.maximum(start - EDGE, 0)
             first = base // LANES
             after = jnp.minimum(first + 1, tiles - 1)
             one = tiled[near + first].astype(jnp.float32)
             two = tiled[near + after].astype(jnp.float32)
-            cuts[j, k] = jnp.where(across >= base % LANES, one, two).astype(cuts.dtype)
-
-    for step in range(n - 1, 0, -1):
-        to = (me + step) % n
-        cut(to)
-        remote(cuts.at[to], cuts_all.at[me], cut_send, cut_recv, "vox", to)
+            span = jnp.where(across >= base % LANES, one, two)
+            spans.append(pltpu.roll(span, (k * SPAN + EDGE - start) & (LANES - 1), 1))
+        for i in range(cuts.shape[1]):
+            packed = None
+            for k in range(slots):
+                begin = k * SPAN - i * LANES
+                if begin + SPAN <= 0 or begin >= LANES:
+                    continue
+                packed = spans[k] if packed is None else jnp.where(across >= begin, spans[k], packed)
+            cuts[j, i] = packed.astype(cuts.dtype)
+
+    order = [peer(me, n, step) for step in range(n - 1, 0, -1)]
+    for some in (order[:2], order[2:]):
+        for to in some:
+            cut(to)
+        for to in some:
+            remote(cuts.at[to], cuts_all.at[me], cut_send, cut_recv, "vox", to)
     cut(me)
     pltpu.make_async_copy(cuts.at[me], cuts_all.at[me], cut_recv).start()
 
@@ -209,45 +233,63 @@
     lane = lane_iota((1, LANES))
 
     sums = (jnp.zeros((HALF, LANES), jnp.float32),) * (slots * 2)
-    for g in range(pieces_all.shape[0]):
+    def gather(j, sums, ks, load):
+        sums = list(sums)
+        for k in ks:
+            number, start = table[j, 0, k], table[j, 1, k]
+            piece = load(j, k, start)
+            turned[j, k] = piece
+            since = (lane - start) & (LANES - 1)
+            spot = number * tiles + lax.shift_right_logical(since + start, 7)
+            target[j, k : k + 1] = jnp.where(since < WIN, spot, -1)
+            key = number * FAR + start
+            for i in range(slots):
+                since = keys[i] - key
+                inside = (since >= 0) & (since < WIN)
+                for h in range(2):
+                    part = piece[h * HALF : (h + 1) * HALF]
+                    sums[2 * i + h] = sums[2 * i + h] + jnp.where(inside, part, 0.0)
+        return tuple(sums)
+
+    def load_pair(j, k, start):
+        return pltpu.roll(pieces_all[k // 2, j], (start + (k % 2) * WIN) & (LANES - 1), 1)
+
+    def load_lone(j, k, start):
+        upper = pltpu.roll(lone_all[j], start & (LANES - 1), 1)
+        lower = pltpu.roll(lone_all[j], (start + WIN) & (LANES - 1), 1)
+        return jnp.concatenate([upper, lower], axis=0)
+
+    for g in range(slots // 2):
         settle(pieces_all.at[g], piece_recv.at[g])
-
-        def gather(j, sums, g=g):
-            sums = list(sums)
-            packed = pieces_all[g, j]
-            for k in range(2 * g, min(2 * g + 2, slots)):
-                number, start = table[j, 0, k], table[j, 1, k]
-                piece = pltpu.roll(packed, (start + (k % 2) * WIN) & (LANES - 1), 1)
-                turned[j, k] = piece
-                since = (lane - start) & (LANES - 1)
-                spot = number * tiles + lax.shift_right_logical(since + start, 7)
-                target[j, k : k + 1] = jnp.where(since < WIN, spot, -1)
-                key = number * FAR + start
-                for i in range(slots):
-                    since = keys[i] - key
-                    inside = (since >= 0) & (since < WIN)
-                    for h in range(2):
-                        part = piece[h * HALF : (h + 1) * HALF]
-                        sums[2 * i + h] = sums[2 * i + h] + jnp.where(inside, part, 0.0)
-            return tuple(sums)
-
-        sums = each(n, gather, sums)
-
-    derived = [stencil(value) for value in sums]
+        sums = each(n, functools.partial(gather, ks=(2 * g, 2 * g + 1), load=load_pair), sums)
+    if slots % 2:
+        settle(lone_all, lone_recv)
+        sums = each(n, functools.partial(gather, ks=(slots - 1,), load=load_lone), sums)
+
+    derived = []
+    for k in range(slots):
+        value = jnp.concatenate([stencil(sums[2 * k]), stencil(sums[2 * k + 1])], axis=0)
+        derived.append(pltpu.roll(value, (LANES + EDGE - starts[k]) & (LANES - 1), 1))
+    wide = lane_iota((SB, LANES))
     settle(cuts_all, cut_recv)
     spreads = []
     for k in range(slots):
-        stripes = [cuts_all[numbers[k] * SB // rows + i, k].astype(jnp.float32) for i in range(strips)]
+        stripes = []
+        for i in range(strips):
+            owner = numbers[k] * SB // rows + i
+            begin, last = k * SPAN, (k + 1) * SPAN - 1
+            stripe = cuts_all[owner, begin // LANES].astype(jnp.float32)
+            if last // LANES > begin // LANES:
+                follow = cuts_all[owner, last // LANES].astype(jnp.float32)
+                stripe = jnp.where(lane_iota((lines, LANES)) >= begin % LANES, stripe, follow)
+            stripes.append(stripe)
         block = stripes[0] if strips == 1 else jnp.concatenate(stripes, axis=0)
-        keep = (times[k] >= 0) & (times[k] < samples) & (jnp.full((HALF, LANES), count[0, 0]) > k)
-        halves = []
-        for h in range(2):
-            rest = jnp.where(keep, derived[2 * k + h] - block[h * HALF : (h + 1) * HALF], 0.0)
-            halves.append(-stencil(rest))
-        window = jnp.concatenate(halves, axis=0)
-        even = pltpu.roll(window, (LANES - starts[k]) & (LANES - 1), 1)
-        odd = pltpu.roll(window, (LANES + WIN - starts[k]) & (LANES - 1), 1)
-        window = jnp.where(left, even, odd)
+        if k:
+            block = pltpu.roll(block, (-k * SPAN) % LANES, 1)
+        time = wide + (starts[k] - EDGE)
+        keep = (time >= 0) & (time < samples) & (jnp.full((SB, LANES), count[0, 0]) > k)
+        window = -stencil(jnp.where(keep, derived[k] - block, 0.0))
+        window = jnp.where(left, ahead(window, EDGE), ahead(window, EDGE - WIN))
         spread = jnp.concatenate([window] * (SB * WIN // LANES), axis=1)
         spreads.append(jnp.where(mask, spread, 0.0).astype(jnp.bfloat16))
     part = None
@@ -299,6 +341,8 @@
     settle(table.at[pl.ds(0, n - 1)], meta_send)
     settle(halo, halo_send)
     settle(pieces_all.at[:, pl.ds(0, n - 1)], piece_send)
+    if slots % 2:
+        settle(lone_all.at[pl.ds(0, n - 1)], piece_send)
     settle(cuts_all.at[pl.ds(0, n - 1)], cut_send)
     settle(parts, grad_recv)
     flat = parts[0]
@@ -327,9 +371,9 @@
     ns = lax.axis_size("sen")
     slots, voxels, cells = weights.shape[2:]
     rows, samples = measured.shape[1:]
-    groups = (slots + 1) // 2
+    pairs = slots // 2
     lines = min(rows, SB)
-    chunks = 4
+    chunks = 2
     vmem = pl.BlockSpec(memory_space=pltpu.VMEM)
     hbm = pl.BlockSpec(memory_space=pltpu.HBM)
     smem = pl.BlockSpec(memory_space=pltpu.SMEM)
@@ -355,10 +399,12 @@
             pltpu.VMEM((2, LANES), jnp.int32),
             pltpu.SMEM((n, 2, LANES), jnp.int32),
             pltpu.VMEM((2,) + image.shape[1:], jnp.float32),
-            pltpu.VMEM((groups, SB, LANES), jnp.float32),
-            pltpu.VMEM((groups, n, SB, LANES), jnp.float32),
-            pltpu.VMEM((n, slots, lines, LANES), jnp.bfloat16),
-            pltpu.VMEM((n, slots, lines, LANES), jnp.bfloat16),
+            pltpu.VMEM((pairs, SB, LANES), jnp.float32),
+            pltpu.VMEM((pairs, n, SB, LANES), jnp.float32),
+            pltpu.VMEM((HALF, LANES), jnp.float32),
+            pltpu.VMEM((n, HALF, LANES), jnp.float32),
+            pltpu.VMEM((n, pl.cdiv(slots * SPAN, LANES), lines, LANES), jnp.bfloat16),
+            pltpu.VMEM((n, pl.cdiv(slots * SPAN, LANES), lines, LANES), jnp.bfloat16),
             pltpu.VMEM((n, slots, SB, LANES), jnp.float32),
             pltpu.VMEM((n, HALF, LANES), jnp.int32),
             pltpu.VMEM((max(rows, SB), samples), jnp.float32),
@@ -371,7 +417,8 @@
             dma,
             dma((2,)),
             dma,
-            dma((groups,)),
+            dma((pairs,)),
+            dma,
             dma,
             dma,
             dma,

time: 21.3 us -> 20.2 us (0.948)
  Pallas kernels: 19.8 us -> 18.7 us
    pallas_call x1, Pallas kernels: 19.1 us -> 18 us  [on_device(): pl.pallas_call(functools.partial(step_kernel, n, ns, slots, chunks), out_...]
where the time goes in v3:
time: 20.2 us; the launch traced here: 20 us
  Pallas kernels  18.7 us (93%)
  between operations  1.29 us (6%)
    pallas_call x1, Pallas kernels, on_device(): pl.pallas_call(functools.partial(step_kernel, n, ns, slots, chunks), out_...  18 us
    pallas_call x1, Pallas kernels, on_device(): pl.pallas_call(store_kernel, out_shape=(shape(image.shape, jnp.float32),...  0.72 us

profile of v3, /device:TPU:0, one launch (start us, length us, event | category | flops | bytes accessed | tf_op | source)
XLA Modules:
  0.0 20.0 jit_solution(3806712363199634556)
XLA Ops:
  1.3 18.0 %step_kernel.1 = (f32[1,2,512]{2,1,0:T(2,128)S(1)}, f32[1,32,2048]{2,1,0:T(8,128)S(1)}) custom-call(f32[1,2,512]{2,1,0:T(2,128)} %image_in.1, bf16[1,1,5,1024,1024]{4,3,2,1,0:T(8,128)(2,1)} %weights.1, s32[1,1,5]{2,1,0:T(1,128)} %ids_in.1, s32[1,1,5]{2,1,0:T(1,128)} %offs_in.1, s32[1,1]{1,0:T(1,128)S(6)} %copy.8.count, bf16[1,32,2048]{2,1,0:T(8,128)(2,1)} %measured_in.1), custom_call_target="tpu_custom_call" | custom-call | tf_op jit(solution)/shard_map/step_kernel/pallas_call | solution.py:386
  19.3 0.7 %store_kernel.1 = (f32[1,2,512]{2,1,0:T(2,128)}, f32[1,32,2048]{2,1,0:T(8,128)}) custom-call(f32[1,2,512]{2,1,0:T(2,128)S(1)} %get-tuple-element.4.image, f32[1,32,2048]{2,1,0:T(8,128)S(1)} %get-tuple-element.5.residual), custom_call_target="tpu_custom_call" | custom-call | tf_op jit(solution)/shard_map/store_kernel/pallas_call | solution.py:433

commit v4 on v3

--- a/solution.py
+++ b/solution.py
@@ -15,6 +15,7 @@
 SPAN = WIN + 2 * EDGE
 FAR = 1 << 16
 UNROLL = 8
+STORES = 4
 
 STEP_SIZE = 0.25
 TV_WEIGHT = 0.3
@@ -95,13 +96,11 @@
     out, residual,
     wbuf, turned_w, image, measured, tiled, ids, offs, meta, table, halo, mine, pieces_all, lone, lone_all,
     cuts, cuts_all, turned, target, signals, grad, parts,
-    wsem, load_sem, meta_send, meta_recv, halo_send, halo_recv, piece_send, piece_recv, lone_recv,
-    cut_send, cut_recv, grad_send, grad_recv,
+    wsem, load_sem, sent, meta_recv, halo_recv, piece_recv, lone_recv, cut_recv, grad_recv,
 ):
     me = lax.axis_index("vox")
     layer = lax.axis_index("sen")
     voxels = weights.shape[3]
-    depth = voxels // chunks
     rows, samples = measured.shape[1:]
     tiles = samples // LANES
     lines = min(rows, SB)
@@ -110,9 +109,9 @@
 
     barrier = pltpu.get_barrier_semaphore()
     for step in range(1, n):
-        pl.semaphore_signal(barrier, inc=1, device_id={"vox": (me + step) % n}, device_id_type=MESH)
+        pl.semaphore_signal(barrier, inc=1, device_id={"vox": peer(me, n, n - step)}, device_id_type=MESH)
     for step in range(1, ns):
-        pl.semaphore_signal(barrier, inc=1, device_id={"sen": (layer + step) % ns}, device_id_type=MESH)
+        pl.semaphore_signal(barrier, inc=1, device_id={"sen": peer(layer, ns, ns - step)}, device_id_type=MESH)
 
     arguments = []
     pairs = ((ids_in, ids), (offs_in, offs), (image_in, image), (measured_in, measured))
@@ -122,11 +121,14 @@
         arguments.append(load)
     loads = []
     for k in range(slots):
-        for q in range(chunks):
+        depth = voxels // chunks[k]
+        strips_of = []
+        for q in range(chunks[k]):
             part = pl.ds(q * depth, depth)
-            load = pltpu.make_async_copy(weights.at[0, 0, k, part], wbuf.at[k, part], wsem.at[k, q])
+            load = pltpu.make_async_copy(weights.at[0, 0, k, part], wbuf.at[k, part], wsem.at[sum(chunks[:k]) + q])
             load.start(priority=1)
-            loads.append(load)
+            strips_of.append(load)
+        loads.append(strips_of)
 
     mask = block_mask(SB * WIN)
     alive = jnp.full((SB, LANES), count[0, 0])
@@ -146,11 +148,11 @@
         ).start()
 
     for step in range(1, n):
-        remote(meta, table.at[me], meta_send, meta_recv, "vox", peer(me, n, n - step))
+        remote(meta, table.at[me], sent, meta_recv, "vox", peer(me, n, n - step))
     pltpu.make_async_copy(meta, table.at[me], meta_recv).start()
     arguments[2].wait()
     for side, to in ((0, (me + 1) % n), (1, (me + n - 1) % n)):
-        remote(image.at[0], halo.at[side], halo_send, halo_recv.at[side], "vox", to)
+        remote(image.at[0], halo.at[side], sent, halo_recv, "vox", to)
     low = image[0].astype(jnp.bfloat16)
     flat = jnp.concatenate([low[r : r + 1] for r in range(low.shape[0])], axis=1)
     flat = jnp.broadcast_to(flat, (SB, voxels))
@@ -160,8 +162,9 @@
 
     def forward(k):
         total = jnp.zeros((SB, SB * WIN), jnp.float32)
-        for q in range(chunks):
-            loads[k * chunks + q].wait()
+        depth = voxels // chunks[k]
+        for q in range(chunks[k]):
+            loads[k][q].wait()
             total = total + jnp.dot(
                 flat[:, q * depth : (q + 1) * depth],
                 wbuf[k, q * depth : (q + 1) * depth],
@@ -176,7 +179,7 @@
 
     def spread_out(src, dst, recv):
         for step in range(1, n):
-            remote(src, dst, piece_send, recv, "vox", peer(me, n, n - step))
+            remote(src, dst, sent, recv, "vox", peer(me, n, n - step))
         pltpu.make_async_copy(src, dst, recv).start()
 
     first = None
@@ -219,7 +222,7 @@
         for to in some:
             cut(to)
         for to in some:
-            remote(cuts.at[to], cuts_all.at[me], cut_send, cut_recv, "vox", to)
+            remote(cuts.at[to], cuts_all.at[me], sent, cut_recv, "vox", to)
     cut(me)
     pltpu.make_async_copy(cuts.at[me], cuts_all.at[me], cut_recv).start()
 
@@ -298,7 +301,7 @@
         part = term if part is None else part + term
     grad[...] = jnp.sum(part, axis=0, keepdims=True)
     for step in range(ns - 1, 0, -1):
-        remote(grad, parts.at[layer], grad_send, grad_recv, "sen", (layer + step) % ns)
+        remote(grad, parts.at[layer], sent, grad_recv, "sen", peer(layer, ns, step))
     pltpu.make_async_copy(grad, parts.at[layer], grad_recv).start()
 
     home = me * rows // SB * tiles
@@ -335,15 +338,14 @@
                 own = jnp.where(which == i * rows, block[i * rows : (i + 1) * rows], own)
             residual[0] = own - measured[0].astype(jnp.float32)
 
-    settle(halo.at[0], halo_recv.at[0])
-    settle(halo.at[1], halo_recv.at[1])
+    settle(halo, halo_recv)
     tv = variation(n, me, image, halo)
-    settle(table.at[pl.ds(0, n - 1)], meta_send)
-    settle(halo, halo_send)
-    settle(pieces_all.at[:, pl.ds(0, n - 1)], piece_send)
+    settle(table.at[pl.ds(0, n - 1)], sent)
+    settle(halo, sent)
+    settle(pieces_all.at[:, pl.ds(0, n - 1)], sent)
     if slots % 2:
-        settle(lone_all.at[pl.ds(0, n - 1)], piece_send)
-    settle(cuts_all.at[pl.ds(0, n - 1)], cut_send)
+        settle(lone_all.at[pl.ds(0, n - 1)], sent)
+    settle(cuts_all.at[pl.ds(0, n - 1)], sent)
     settle(parts, grad_recv)
     flat = parts[0]
     for index in range(1, ns):
@@ -353,15 +355,18 @@
     for r in range(volume.shape[0]):
         total = flat[:, r * width : (r + 1) * width]
         out[0, r : r + 1] = volume[r : r + 1] - STEP_SIZE * (total + TV_WEIGHT * tv[r : r + 1])
-    settle(parts.at[pl.ds(0, ns - 1)], grad_send)
+    settle(parts.at[pl.ds(0, ns - 1)], sent)
 
 
 def store_kernel(image, residual, image_out, residual_out, sem):
-    copies = []
-    for i, (src, dst) in enumerate(((residual, residual_out), (image, image_out))):
-        copy = pltpu.make_async_copy(src, dst, sem.at[i])
+    rows = residual.shape[1]
+    depth = rows // STORES if rows % (STORES * HALF) == 0 else rows
+    copies = [pltpu.make_async_copy(image, image_out, sem.at[0])]
+    for i, r in enumerate(range(0, rows, depth)):
+        part = pl.ds(r, depth)
+        copies.append(pltpu.make_async_copy(residual.at[:, part], residual_out.at[:, part], sem.at[1 + i]))
+    for copy in copies:
         copy.start()
-        copies.append(copy)
     for copy in copies:
         copy.wait()
 
@@ -373,7 +378,7 @@
     rows, samples = measured.shape[1:]
     pairs = slots // 2
     lines = min(rows, SB)
-    chunks = 2
+    chunks = (1,) * (slots - 1) + (4,)
     vmem = pl.BlockSpec(memory_space=pltpu.VMEM)
     hbm = pl.BlockSpec(memory_space=pltpu.HBM)
     smem = pl.BlockSpec(memory_space=pltpu.SMEM)
@@ -410,16 +415,12 @@
             pltpu.VMEM((max(rows, SB), samples), jnp.float32),
             pltpu.VMEM((1, voxels), jnp.float32),
             pltpu.VMEM((ns, 1, voxels), jnp.float32),
-            dma((slots, chunks)),
+            dma((sum(chunks),)),
             dma((4,)),
             dma,
             dma,
             dma,
-            dma((2,)),
-            dma,
             dma((pairs,)),
-            dma,
-            dma,
             dma,
             dma,
             dma,
@@ -435,7 +436,7 @@
         out_shape=(shape(image.shape, jnp.float32), shape(measured.shape, jnp.float32)),
         in_specs=[vmem, vmem],
         out_specs=(hbm, hbm),
-        scratch_shapes=[dma((2,))],
+        scratch_shapes=[dma((1 + STORES,))],
         compiler_params=pltpu.CompilerParams(vmem_limit_bytes=1 << 20),
         name="store_kernel",
     )(image_next, residual)

time: 20.2 us -> 20 us (0.990)
  no operation moved by 1% of the time
where the time goes in v4:
time: 20 us; the launch traced here: 19.8 us
  Pallas kernels  18.5 us (92%)
  between operations  1.29 us (6%)
    pallas_call x1, Pallas kernels, on_device(): pl.pallas_call(functools.partial(step_kernel, n, ns, slots, chunks), out_...  17.8 us
    pallas_call x1, Pallas kernels, on_device(): pl.pallas_call(store_kernel, out_shape=(shape(image.shape, jnp.float32),...  0.74 us

profile of v4, /device:TPU:0, one launch (start us, length us, event | category | flops | bytes accessed | tf_op | source)
XLA Modules:
  0.0 19.8 jit_solution(16622274158093767054)
XLA Ops:
  1.3 17.8 %step_kernel.1 = (f32[1,2,512]{2,1,0:T(2,128)S(1)}, f32[1,32,2048]{2,1,0:T(8,128)S(1)}) custom-call(f32[1,2,512]{2,1,0:T(2,128)} %image_in.1, bf16[1,1,5,1024,1024]{4,3,2,1,0:T(8,128)(2,1)} %weights.1, s32[1,1,5]{2,1,0:T(1,128)} %ids_in.1, s32[1,1,5]{2,1,0:T(1,128)} %offs_in.1, s32[1,1]{1,0:T(1,128)S(6)} %copy.8.count, bf16[1,32,2048]{2,1,0:T(8,128)(2,1)} %measured_in.1), custom_call_target="tpu_custom_call" | custom-call | tf_op jit(solution)/shard_map/step_kernel/pallas_call | solution.py:391
  19.1 0.7 %store_kernel.1 = (f32[1,2,512]{2,1,0:T(2,128)}, f32[1,32,2048]{2,1,0:T(8,128)}) custom-call(f32[1,2,512]{2,1,0:T(2,128)S(1)} %get-tuple-element.4.image, f32[1,32,2048]{2,1,0:T(8,128)S(1)} %get-tuple-element.5.residual), custom_call_target="tpu_custom_call" | custom-call | tf_op jit(solution)/shard_map/store_kernel/pallas_call | solution.py:434

commit v5 on v4

--- a/solution.py
+++ b/solution.py
@@ -15,6 +15,7 @@
 SPAN = WIN + 2 * EDGE
 FAR = 1 << 16
 UNROLL = 8
+EARLY = 2
 STORES = 4
 
 STEP_SIZE = 0.25
@@ -52,8 +53,8 @@
     return lane_iota((SB, width)) // WIN == row
 
 
-def peer(me, count, step):
-    return me ^ step if count & (count - 1) == 0 else (me + step) % count
+def peer(me, count, i):
+    return i + (i + count - me) // count
 
 
 def each(count, body, carry):
@@ -108,10 +109,10 @@
     per = max(rows // SB, 1)
 
     barrier = pltpu.get_barrier_semaphore()
-    for step in range(1, n):
-        pl.semaphore_signal(barrier, inc=1, device_id={"vox": peer(me, n, n - step)}, device_id_type=MESH)
-    for step in range(1, ns):
-        pl.semaphore_signal(barrier, inc=1, device_id={"sen": peer(layer, ns, ns - step)}, device_id_type=MESH)
+    for i in range(n - 1):
+        pl.semaphore_signal(barrier, inc=1, device_id={"vox": peer(me, n, i)}, device_id_type=MESH)
+    for i in range(ns - 1):
+        pl.semaphore_signal(barrier, inc=1, device_id={"sen": peer(layer, ns, i)}, device_id_type=MESH)
 
     arguments = []
     pairs = ((ids_in, ids), (offs_in, offs), (image_in, image), (measured_in, measured))
@@ -147,8 +148,8 @@
             device_id={axis: to}, device_id_type=MESH,
         ).start()
 
-    for step in range(1, n):
-        remote(meta, table.at[me], sent, meta_recv, "vox", peer(me, n, n - step))
+    for i in range(n - 1):
+        remote(meta, table.at[me], sent, meta_recv, "vox", peer(me, n, i))
     pltpu.make_async_copy(meta, table.at[me], meta_recv).start()
     arguments[2].wait()
     for side, to in ((0, (me + 1) % n), (1, (me + n - 1) % n)):
@@ -178,8 +179,8 @@
         return jnp.where(alive > k, tile, 0.0)
 
     def spread_out(src, dst, recv):
-        for step in range(1, n):
-            remote(src, dst, sent, recv, "vox", peer(me, n, n - step))
+        for i in range(n - 1):
+            remote(src, dst, sent, recv, "vox", peer(me, n, i))
         pltpu.make_async_copy(src, dst, recv).start()
 
     first = None
@@ -192,6 +193,16 @@
             lone[...] = jnp.where(left[0:HALF], tile[0:HALF], tile[HALF:SB])
             spread_out(lone, lone_all.at[me], lone_recv)
         first = tile
+
+    def transpose(ks):
+        for k in ks:
+            turned_w[k] = wbuf[k].T
+
+    early = range(min(EARLY, slots))
+
+    @pl.when(me < n // 4)
+    def _():
+        transpose(early)
 
     settle(table, meta_recv)
 
@@ -217,8 +228,8 @@
                 packed = spans[k] if packed is None else jnp.where(across >= begin, spans[k], packed)
             cuts[j, i] = packed.astype(cuts.dtype)
 
-    order = [peer(me, n, step) for step in range(n - 1, 0, -1)]
-    for some in (order[:2], order[2:]):
+    order = [peer(me, n, i) for i in range(n - 1)]
+    for some in (order[:1], order[1:]):
         for to in some:
             cut(to)
         for to in some:
@@ -226,8 +237,11 @@
     cut(me)
     pltpu.make_async_copy(cuts.at[me], cuts_all.at[me], cut_recv).start()
 
-    for k in range(slots):
-        turned_w[k] = wbuf[k].T
+    @pl.when(me >= n // 4)
+    def _():
+        transpose(early)
+
+    transpose(range(len(early), slots))
 
     numbers = [table[me, 0, k] for k in range(slots)]
     starts = [table[me, 1, k] for k in range(slots)]
@@ -272,7 +286,7 @@
     derived = []
     for k in range(slots):
         value = jnp.concatenate([stencil(sums[2 * k]), stencil(sums[2 * k + 1])], axis=0)
-        derived.append(pltpu.roll(value, (LANES + EDGE - starts[k]) & (LANES - 1), 1))
+        derived.append(pltpu.roll(value, (k * SPAN + EDGE - starts[k]) & (LANES - 1), 1))
     wide = lane_iota((SB, LANES))
     settle(cuts_all, cut_recv)
     spreads = []
@@ -287,12 +301,11 @@
                 stripe = jnp.where(lane_iota((lines, LANES)) >= begin % LANES, stripe, follow)
             stripes.append(stripe)
         block = stripes[0] if strips == 1 else jnp.concatenate(stripes, axis=0)
-        if k:
-            block = pltpu.roll(block, (-k * SPAN) % LANES, 1)
-        time = wide + (starts[k] - EDGE)
+        time = ((wide - k * SPAN) & (LANES - 1)) + (starts[k] - EDGE)
         keep = (time >= 0) & (time < samples) & (jnp.full((SB, LANES), count[0, 0]) > k)
         window = -stencil(jnp.where(keep, derived[k] - block, 0.0))
-        window = jnp.where(left, ahead(window, EDGE), ahead(window, EDGE - WIN))
+        turn = k * SPAN + EDGE
+        window = jnp.where(left, ahead(window, turn), ahead(window, turn - WIN))
         spread = jnp.concatenate([window] * (SB * WIN // LANES), axis=1)
         spreads.append(jnp.where(mask, spread, 0.0).astype(jnp.bfloat16))
     part = None
@@ -300,8 +313,8 @@
         term = jnp.dot(spreads[k], turned_w[k], preferred_element_type=jnp.float32)
         part = term if part is None else part + term
     grad[...] = jnp.sum(part, axis=0, keepdims=True)
-    for step in range(ns - 1, 0, -1):
-        remote(grad, parts.at[layer], sent, grad_recv, "sen", peer(layer, ns, step))
+    for i in range(ns - 1):
+        remote(grad, parts.at[layer], sent, grad_recv, "sen", peer(layer, ns, i))
     pltpu.make_async_copy(grad, parts.at[layer], grad_recv).start()
 
     home = me * rows // SB * tiles

time: 20 us -> 19.9 us (level)
  no operation moved by 1% of the time
where the time goes in v5:
time: 19.9 us; the launch traced here: 19.7 us
  Pallas kernels  18.5 us (93%)
  between operations  1.29 us (6%)
    pallas_call x1, Pallas kernels, on_device(): pl.pallas_call(functools.partial(step_kernel, n, ns, slots, chunks), out_...  17.7 us
    pallas_call x1, Pallas kernels, on_device(): pl.pallas_call(store_kernel, out_shape=(shape(image.shape, jnp.float32),...  0.74 us

profile of v5, /device:TPU:0, one launch (start us, length us, event | category | flops | bytes accessed | tf_op | source)
XLA Modules:
  0.0 19.7 jit_solution(17244576973289187456)
XLA Ops:
  1.3 17.7 %step_kernel.1 = (f32[1,2,512]{2,1,0:T(2,128)S(1)}, f32[1,32,2048]{2,1,0:T(8,128)S(1)}) custom-call(f32[1,2,512]{2,1,0:T(2,128)} %image_in.1, bf16[1,1,5,1024,1024]{4,3,2,1,0:T(8,128)(2,1)} %weights.1, s32[1,1,5]{2,1,0:T(1,128)} %ids_in.1, s32[1,1,5]{2,1,0:T(1,128)} %offs_in.1, s32[1,1]{1,0:T(1,128)S(6)} %copy.8.count, bf16[1,32,2048]{2,1,0:T(8,128)(2,1)} %measured_in.1), custom_call_target="tpu_custom_call" | custom-call | tf_op jit(solution)/shard_map/step_kernel/pallas_call | solution.py:404
  19.0 0.7 %store_kernel.1 = (f32[1,2,512]{2,1,0:T(2,128)}, f32[1,32,2048]{2,1,0:T(8,128)}) custom-call(f32[1,2,512]{2,1,0:T(2,128)S(1)} %get-tuple-element.4.image, f32[1,32,2048]{2,1,0:T(8,128)S(1)} %get-tuple-element.5.residual), custom_call_target="tpu_custom_call" | custom-call | tf_op jit(solution)/shard_map/store_kernel/pallas_call | solution.py:447

commit v6 on v5

--- a/solution.py
+++ b/solution.py
@@ -148,7 +148,7 @@
             device_id={axis: to}, device_id_type=MESH,
         ).start()
 
-    for i in range(n - 1):
+    for i in reversed(range(n - 1)):
         remote(meta, table.at[me], sent, meta_recv, "vox", peer(me, n, i))
     pltpu.make_async_copy(meta, table.at[me], meta_recv).start()
     arguments[2].wait()

time: 19.9 us -> 19.8 us (level)
  no operation moved by 1% of the time
where the time goes in v6:
time: 19.8 us; the launch traced here: 19.7 us
  Pallas kernels  18.4 us (93%)
  between operations  1.29 us (7%)
    pallas_call x1, Pallas kernels, on_device(): pl.pallas_call(functools.partial(step_kernel, n, ns, slots, chunks), out_...  17.6 us
    pallas_call x1, Pallas kernels, on_device(): pl.pallas_call(store_kernel, out_shape=(shape(image.shape, jnp.float32),...  0.74 us

profile of v6, /device:TPU:0, one launch (start us, length us, event | category | flops | bytes accessed | tf_op | source)
XLA Modules:
  0.0 19.7 jit_solution(4701416413007638376)
XLA Ops:
  1.3 17.6 %step_kernel.1 = (f32[1,2,512]{2,1,0:T(2,128)S(1)}, f32[1,32,2048]{2,1,0:T(8,128)S(1)}) custom-call(f32[1,2,512]{2,1,0:T(2,128)} %image_in.1, bf16[1,1,5,1024,1024]{4,3,2,1,0:T(8,128)(2,1)} %weights.1, s32[1,1,5]{2,1,0:T(1,128)} %ids_in.1, s32[1,1,5]{2,1,0:T(1,128)} %offs_in.1, s32[1,1]{1,0:T(1,128)S(6)} %copy.8.count, bf16[1,32,2048]{2,1,0:T(8,128)(2,1)} %measured_in.1), custom_call_target="tpu_custom_call" | custom-call | tf_op jit(solution)/shard_map/step_kernel/pallas_call | solution.py:404
  18.9 0.7 %store_kernel.1 = (f32[1,2,512]{2,1,0:T(2,128)}, f32[1,32,2048]{2,1,0:T(8,128)}) custom-call(f32[1,2,512]{2,1,0:T(2,128)S(1)} %get-tuple-element.4.image, f32[1,32,2048]{2,1,0:T(8,128)S(1)} %get-tuple-element.5.residual), custom_call_target="tpu_custom_call" | custom-call | tf_op jit(solution)/shard_map/store_kernel/pallas_call | solution.py:447

commit v7 on v6

--- a/solution.py
+++ b/solution.py
@@ -16,7 +16,7 @@
 FAR = 1 << 16
 UNROLL = 8
 EARLY = 2
-STORES = 4
+STORES = 1
 
 STEP_SIZE = 0.25
 TV_WEIGHT = 0.3
@@ -391,7 +391,7 @@
     rows, samples = measured.shape[1:]
     pairs = slots // 2
     lines = min(rows, SB)
-    chunks = (1,) * (slots - 1) + (4,)
+    chunks = (1,) * (slots - 1) + (2,)
     vmem = pl.BlockSpec(memory_space=pltpu.VMEM)
     hbm = pl.BlockSpec(memory_space=pltpu.HBM)
     smem = pl.BlockSpec(memory_space=pltpu.SMEM)

time: 19.8 us -> 19.8 us (level)
  no operation moved by 1% of the time
where the time goes in v7:
time: 19.8 us; the launch traced here: 19.6 us
  Pallas kernels  18.4 us (93%)
  between operations  1.29 us (7%)
    pallas_call x1, Pallas kernels, on_device(): pl.pallas_call(functools.partial(step_kernel, n, ns, slots, chunks), out_...  17.6 us
    pallas_call x1, Pallas kernels, on_device(): pl.pallas_call(store_kernel, out_shape=(shape(image.shape, jnp.float32),...  0.73 us

profile of v7, /device:TPU:0, one launch (start us, length us, event | category | flops | bytes accessed | tf_op | source)
XLA Modules:
  0.0 19.6 jit_solution(8158164652781416614)
XLA Ops:
  1.3 17.6 %step_kernel.1 = (f32[1,2,512]{2,1,0:T(2,128)S(1)}, f32[1,32,2048]{2,1,0:T(8,128)S(1)}) custom-call(f32[1,2,512]{2,1,0:T(2,128)} %image_in.1, bf16[1,1,5,1024,1024]{4,3,2,1,0:T(8,128)(2,1)} %weights.1, s32[1,1,5]{2,1,0:T(1,128)} %ids_in.1, s32[1,1,5]{2,1,0:T(1,128)} %offs_in.1, s32[1,1]{1,0:T(1,128)S(6)} %copy.8.count, bf16[1,32,2048]{2,1,0:T(8,128)(2,1)} %measured_in.1), custom_call_target="tpu_custom_call" | custom-call | tf_op jit(solution)/shard_map/step_kernel/pallas_call | solution.py:404
  18.9 0.7 %store_kernel.1 = (f32[1,2,512]{2,1,0:T(2,128)}, f32[1,32,2048]{2,1,0:T(8,128)}) custom-call(f32[1,2,512]{2,1,0:T(2,128)S(1)} %get-tuple-element.4.image, f32[1,32,2048]{2,1,0:T(8,128)S(1)} %get-tuple-element.5.residual), custom_call_target="tpu_custom_call" | custom-call | tf_op jit(solution)/shard_map/store_kernel/pallas_call | solution.py:447

commit v8 on v7

--- a/solution.py
+++ b/solution.py
@@ -117,7 +117,7 @@
     arguments = []
     pairs = ((ids_in, ids), (offs_in, offs), (image_in, image), (measured_in, measured))
     for i, (src, dst) in enumerate(pairs):
-        load = pltpu.make_async_copy(src, dst, load_sem.at[i])
+        load = pltpu.make_async_copy(src, dst, load_sem.at[i // 2])
         load.start()
         arguments.append(load)
     loads = []
@@ -152,12 +152,12 @@
         remote(meta, table.at[me], sent, meta_recv, "vox", peer(me, n, i))
     pltpu.make_async_copy(meta, table.at[me], meta_recv).start()
     arguments[2].wait()
+    arguments[3].wait()
     for side, to in ((0, (me + 1) % n), (1, (me + n - 1) % n)):
         remote(image.at[0], halo.at[side], sent, halo_recv, "vox", to)
     low = image[0].astype(jnp.bfloat16)
     flat = jnp.concatenate([low[r : r + 1] for r in range(low.shape[0])], axis=1)
     flat = jnp.broadcast_to(flat, (SB, voxels))
-    arguments[3].wait()
     for i in range(per * tiles):
         tiled[i] = measured[0, i // tiles * SB : i // tiles * SB + lines, i % tiles * LANES : (i % tiles + 1) * LANES]
 
@@ -429,7 +429,7 @@
             pltpu.VMEM((1, voxels), jnp.float32),
             pltpu.VMEM((ns, 1, voxels), jnp.float32),
             dma((sum(chunks),)),
-            dma((4,)),
+            dma((2,)),
             dma,
             dma,
             dma,

time: 19.8 us -> 19.8 us (level)
  no operation moved by 1% of the time
where the time goes in v8:
time: 19.8 us; the launch traced here: 19.6 us
  Pallas kernels  18.3 us (92%)
  between operations  1.29 us (7%)
    pallas_call x1, Pallas kernels, on_device(): pl.pallas_call(functools.partial(step_kernel, n, ns, slots, chunks), out_...  17.6 us
    pallas_call x1, Pallas kernels, on_device(): pl.pallas_call(store_kernel, out_shape=(shape(image.shape, jnp.float32),...  0.73 us

profile of v8, /device:TPU:0, one launch (start us, length us, event | category | flops | bytes accessed | tf_op | source)
XLA Modules:
  0.0 19.6 jit_solution(14880270355143949650)
XLA Ops:
  1.3 17.6 %step_kernel.1 = (f32[1,2,512]{2,1,0:T(2,128)S(1)}, f32[1,32,2048]{2,1,0:T(8,128)S(1)}) custom-call(f32[1,2,512]{2,1,0:T(2,128)} %image_in.1, bf16[1,1,5,1024,1024]{4,3,2,1,0:T(8,128)(2,1)} %weights.1, s32[1,1,5]{2,1,0:T(1,128)} %ids_in.1, s32[1,1,5]{2,1,0:T(1,128)} %offs_in.1, s32[1,1]{1,0:T(1,128)S(6)} %copy.8.count, bf16[1,32,2048]{2,1,0:T(8,128)(2,1)} %measured_in.1), custom_call_target="tpu_custom_call" | custom-call | tf_op jit(solution)/shard_map/step_kernel/pallas_call | solution.py:404
  18.9 0.7 %store_kernel.1 = (f32[1,2,512]{2,1,0:T(2,128)}, f32[1,32,2048]{2,1,0:T(8,128)}) custom-call(f32[1,2,512]{2,1,0:T(2,128)S(1)} %get-tuple-element.4.image, f32[1,32,2048]{2,1,0:T(8,128)S(1)} %get-tuple-element.5.residual), custom_call_target="tpu_custom_call" | custom-call | tf_op jit(solution)/shard_map/store_kernel/pallas_call | solution.py:447
